TPU v7x, 256 devices: a whole 4x4x8 slice. The times are simulated.
256 devices in a mesh: dp: 32 (over z, y), mp: 8 (over x, core).
Axes of the slice: x: 4, y: 4, z: 8, core: 2. Of those that a mesh axis runs over, the one named last changes fastest.
Arguments:
- queries: bfloat16 [256, 64, 128], P('dp', 'mp'), may hold values from -140 to 140
- resident_cache: bfloat16 [256, 256, 8, 128], P('dp', None, 'mp'), may hold values from -6 to 6
- overflow_cache: bfloat16 [32, 32, 2, 128, 8, 128], P('dp', None, None, None, 'mp'), may hold values from -6 to 6
- key_up_weight: bfloat16 [8, 64, 128], P('mp'), may hold values from -0.75 to 0.75
- value_up_weight: bfloat16 [8, 64, 128], P('mp'), may hold values from -0.75 to 0.75
- lengths: int32 [256], replicated, may hold values from 257 to 1024
- routes: int32 [256, 6, 1], replicated, may hold values from 0 to 31; in each aligned block of 48 rows (0 to 47, 48 to 95, ..., all dimensions but the last counted through in order) at most 2 rows name the same one
- out_weight: bfloat16 [8192, 8192], P('mp', 'dp'), may hold values from -0.0625 to 0.0625
Outputs:
- mixed_out: bfloat16 [256, 8192], P('mp', 'dp')
Inputs may be any that keep to these rules, and one draw needn't show every extreme that they name: Among the 48 entries of one sequence group (sequences s with the same s // 8) no group is named more than 2 times; the page named by routes[s, j, 0] lies in the slots of that holding group kept for the group s // 8, at the slot given by ranking. Slots that no entry names hold data that no output reads.
All inputs are finite; a program needn't handle non-finite values.
Results may differ from a plain program's by a relative error of at most 0.0049.
Values may be sent and summed in bfloat16 or wider, within the bound.
A program may use at most 64 MiB of HBM per device.

v0:
```python
import math

import jax
import jax.numpy as jnp
from jax import lax
from jax.sharding import PartitionSpec as P

very_low = -1e30


def copy_for_each(x, axis):
    peers = lax.axis_size(axis)
    return lax.all_to_all(jnp.broadcast_to(x[None], (peers, *x.shape)), axis, 0, 0, tiled=True)


def in_order(tiles, dim):
    tiles = jnp.moveaxis(tiles, 0, dim)
    shape = tiles.shape
    return tiles.reshape(*shape[:dim], shape[dim] * shape[dim + 1], *shape[dim + 2 :])


def collect(x, axis, dim):
    tiles = copy_for_each(x, axis)
    return in_order(tiles, dim)


def sent_together(arrays, axis, split_dim, concat_dim, along):
    columns = [a.reshape(*a.shape[:along], -1) for a in arrays]
    both = jnp.concatenate(columns, axis=along)
    whole, at, done = (
        lax.all_to_all(both, axis, split_axis=split_dim, concat_axis=concat_dim, tiled=True),
        0,
        [],
    )
    for a, column in zip(arrays, columns):
        piece = whole[..., at : at + column.shape[along]]
        done.append(piece.reshape(*piece.shape[:along], *a.shape[along:]))
        at += column.shape[along]
    return tuple(done)


def split_up(x, dim, peers):
    shape = x.shape
    tiles = x.reshape(*shape[:dim], peers, shape[dim] // peers, *shape[dim + 1 :])
    return jnp.moveaxis(tiles, dim, 0)


def sum_at_owner(x, axis, dim):
    peers = lax.axis_size(axis)
    tiles = lax.all_to_all(split_up(x, dim, peers), axis, 0, 0, tiled=True)
    return jnp.sum(tiles, axis=0)


def spill_ranks(targets):
    entry_count = targets.shape[-1]
    position = jnp.arange(entry_count, dtype=jnp.int32)
    same_target = targets[..., :, None] == targets[..., None, :]
    earlier = position[None, :] < position[:, None]
    return jnp.sum((same_target & earlier).astype(jnp.int32), axis=-1)


def slot_entries(targets, ranking, wanted, slot_count):
    choices_row = jnp.arange(slot_count, dtype=jnp.int32)
    matches = (targets[:, None, :] == wanted) & (ranking[:, None, :] == choices_row[None, :, None])
    position = jnp.arange(targets.shape[-1], dtype=jnp.int32)
    entries = jnp.sum(jnp.where(matches, position, 0), axis=-1)
    present = jnp.any(matches, axis=-1)
    return (entries, present)


def page_partials(latent_vector, query_rows, token_valid, key_up_weight, value_up_weight):
    key_width = key_up_weight.shape[1]
    score_scale = 1.0 / math.sqrt(key_up_weight.shape[2])
    highest = lax.Precision.HIGHEST
    folded = jnp.einsum(
        "pkgd,krd->pkgr", query_rows, key_up_weight, preferred_element_type=jnp.float32
    )
    scores = jnp.einsum(
        "pkgr,ptkr->pkgt",
        folded,
        latent_vector[..., :key_width].astype(jnp.float32),
        precision=highest,
    )
    scores = scores * score_scale
    token_mask = token_valid[:, None, None, :]
    scores = jnp.where(token_mask, scores, very_low)
    peak_score = jnp.max(scores, axis=-1)
    weights = jnp.where(token_mask, jnp.exp(scores - peak_score[..., None]), 0.0)
    weight_sum = jnp.sum(weights, axis=-1)
    mixed_latent = jnp.einsum(
        "pkgt,ptkr->pkgr",
        weights,
        latent_vector[..., key_width:].astype(jnp.float32),
        precision=highest,
    )
    weighted = jnp.einsum(
        "pkgr,krd->pkgd", mixed_latent, value_up_weight.astype(jnp.float32), precision=highest
    )
    return (peak_score, weight_sum, weighted)


def merge_parts(home_parts, far_parts, own_sequence, present):
    highest = lax.Precision.HIGHEST
    home_peak, home_sum, home_weighted = home_parts
    far_peak, far_sum, far_weighted = far_parts
    seq_count = home_peak.shape[0]
    member = (own_sequence[:, None] == jnp.arange(seq_count, dtype=jnp.int32)[None, :]) & present[
        :, None
    ]
    member_weight = member.astype(jnp.float32)
    far_best = jnp.max(jnp.where(member[:, :, None, None], far_peak[:, None], very_low), axis=0)
    highest_peak = jnp.maximum(home_peak, far_best)
    item_peak = jnp.einsum("is,skg->ikg", member_weight, highest_peak, precision=highest)
    far_factor = jnp.where(present[:, None, None], jnp.exp(far_peak - item_peak), 0.0)
    home_factor = jnp.exp(home_peak - highest_peak)
    weight_sum = home_sum * home_factor + jnp.einsum(
        "is,ikg->skg", member_weight, far_sum * far_factor, precision=highest
    )
    weighted = home_weighted * home_factor[..., None] + jnp.einsum(
        "is,ikgd->skgd", member_weight, far_weighted * far_factor[..., None], precision=highest
    )
    return weighted / weight_sum[..., None]


def body(
    queries,
    resident_cache,
    overflow_cache,
    key_up_weight,
    value_up_weight,
    lengths,
    routes,
    out_weight,
):
    seq_dev, head_dev, head_size = queries.shape
    kv_heads = key_up_weight.shape[0]
    head_cluster = head_dev // kv_heads
    group_count = lax.axis_size("dp")
    own_group = lax.axis_index("dp")
    slot_count = overflow_cache.shape[2]
    page_size = overflow_cache.shape[3]
    home_tokens = resident_cache.shape[1]
    tail_pages = routes.shape[1]
    item_count = group_count * slot_count
    targets_all = routes[:, :, 0].reshape(group_count, seq_dev * tail_pages)
    ranking_all = spill_ranks(targets_all)
    own_lengths = lax.dynamic_slice_in_dim(lengths, own_group * seq_dev, seq_dev)
    local_queries = queries.reshape(seq_dev, kv_heads, head_cluster, head_size)
    home_valid = jnp.arange(home_tokens, dtype=jnp.int32)[None, :] < own_lengths[:, None]
    home_parts = page_partials(
        resident_cache, local_queries, home_valid, key_up_weight, value_up_weight
    )
    own_targets = lax.dynamic_slice_in_dim(targets_all, own_group, 1)
    own_ranking = lax.dynamic_slice_in_dim(ranking_all, own_group, 1)
    holders = jnp.arange(group_count, dtype=jnp.int32)[:, None, None]
    own_entries, own_present = slot_entries(own_targets, own_ranking, holders, slot_count)
    own_sequence = (own_entries // tail_pages).reshape(item_count)
    page_offsets = jnp.arange(page_size, dtype=jnp.int32)
    all_queries = collect(queries, "dp", 0)
    entries, present = slot_entries(targets_all, ranking_all, own_group, slot_count)
    sources = jnp.arange(group_count, dtype=jnp.int32)[:, None]
    sequence = sources * seq_dev + entries // tail_pages
    first_token = home_tokens + entries % tail_pages * page_size
    item_valid = (first_token[..., None] + page_offsets < lengths[sequence][..., None]) & present[
        ..., None
    ]
    item_queries = all_queries[sequence.reshape(item_count)].reshape(
        item_count, kv_heads, head_cluster, head_size
    )
    latent_vector = overflow_cache.reshape(item_count, page_size, kv_heads, -1)
    peak_score, weight_sum, weighted = page_partials(
        latent_vector,
        item_queries,
        item_valid.reshape(item_count, page_size),
        key_up_weight,
        value_up_weight,
    )
    peak_score, weight_sum, weighted = sent_together(
        (
            peak_score.reshape(group_count, slot_count, kv_heads, head_cluster),
            weight_sum.reshape(group_count, slot_count, kv_heads, head_cluster),
            weighted.reshape(group_count, slot_count, kv_heads, head_cluster, head_size),
        ),
        "dp",
        0,
        0,
        4,
    )
    far_parts = (
        peak_score.reshape(item_count, kv_heads, head_cluster),
        weight_sum.reshape(item_count, kv_heads, head_cluster),
        weighted.reshape(item_count, kv_heads, head_cluster, head_size),
    )
    attended = merge_parts(home_parts, far_parts, own_sequence, own_present.reshape(item_count))
    attended = attended.reshape(seq_dev, head_dev * head_size).astype(jnp.bfloat16)
    partial_out = jnp.dot(
        collect(attended, "dp", 0), out_weight, preferred_element_type=jnp.float32
    )
    return sum_at_owner(partial_out, "mp", 0).astype(jnp.bfloat16)


def solution(mesh):
    placed = (
        P("dp", "mp", None),
        P("dp", None, "mp", None),
        P("dp", None, None, None, "mp", None),
        P("mp", None, None),
        P("mp", None, None),
        P(),
        P(),
        P("mp", "dp"),
    )
    return jax.shard_map(body, mesh=mesh, in_specs=placed, out_specs=P("mp", "dp"), check_vma=False)
```

profile of v0, /device:TPU:1, one launch (start us, length us, event | category | flops | bytes accessed | tf_op | source)
XLA Modules:
  0.0 95.8 jit_solution(13267951427326612876)
XLA Ops:
  0.0 1.7 %broadcast_in_dim.126 = bf16[32,8,8,128]{3,2,1,0:T(8,128)(2,1)} broadcast(bf16[8,8,128]{2,1,0:T(8,128)(2,1)} %param.8), dimensions={1,2,3} | broadcast | bytes 540672 | tf_op jit(solution)/shard_map/broadcast_in_dim | solution.py:13
  1.7 12.2 %all-to-all-start = ((bf16[32,8,8,128]{3,2,1,0:T(8,128)(2,1)}), bf16[32,8,8,128]{3,2,1,0:T(8,128)(2,1)}, u32[]{:S(2)}, u32[]{:S(2)}) async-start(bf16[32,8,8,128]{3,2,1,0:T(8,128)(2,1)} %broadcast_in_dim.126), calls=%async_computation | async-start | bytes 1048576 | tf_op jit(solution)/shard_map/all_to_all | solution.py:13
  13.9 0.8 copy.64
  14.9 0.8 convert_reduce_fusion
  16.2 0.8 dynamic_slice.11
  17.4 0.1 and.116
  18.4 0.8 gather_fusion
  19.7 3.3 %copy.73 = bf16[1,32,2,128,1,128]{3,5,2,1,4,0:T(8,128)(2,1)S(1)} copy(bf16[1,32,2,128,1,128]{5,3,4,2,1,0:T(8,128)(2,1)} %param.10) | data formatting | bytes 4194304 | tf_op args[2]
  23.0 0.6 fusion.52
  23.5 0.2 fusion.24
  23.9 6.3 %all-to-all-done = bf16[32,8,8,128]{3,2,1,0:T(8,128)(2,1)} async-done(((bf16[32,8,8,128]{3,2,1,0:T(8,128)(2,1)}), bf16[32,8,8,128]{3,2,1,0:T(8,128)(2,1)}, u32[]{:S(2)}, u32[]{:S(2)}) %all-to-all-start) | async-done | bytes 524320 | tf_op jit(solution)/shard_map/all_to_all | solution.py:13
  30.2 1.7 %gather_fusion.1 = bf16[64,8,128]{2,1,0:T(8,128)(2,1)S(1)} fusion(bf16[256,8,128]{2,1,0:T(8,128)(2,1)} %bitcast.15, s32[1024]{0:T(1024)S(1)} %pad_clamp_fusion), kind=kCustom, calls=%fused_computation.1 | custom fusion | bytes 262400 | tf_op jit(solution)/shard_map/gather | solution.py:167
  31.8 0.2 fusion.35
  32.0 1.0 %fusion.53 = (f32[64,8]{1,0:T(8,128)S(1)}, f32[64,8,128]{2,1,0:T(8,128)S(1)}) fusion(f32[64,8,64]{2,1,0:T(8,128)S(1)} %fusion.35, bf16[64,128,1,128]{1,3,0,2:T(8,128)(2,1)S(1)} %bitcast.119, pred[64,128]{1,0:T(8,128)(4,1)S(1)} %fusion.30), kind=kOutput, calls=%fused_computation.97 | convolution fusion | flops 50527744 | bytes 1583104 | tf_op jit(solution)/shard_map/pkgr,ptkr->pkgt/dot_general | solution.py:78
  33.0 1.8 %fusion.10 = f32[64,8,64]{2,1,0:T(8,128)S(1)} fusion(bf16[64,128,1,128]{1,3,0,2:T(8,128)(2,1)S(1)} %bitcast.120, f32[64,8,128]{2,1,0:T(8,128)S(1)} %get-tuple-element.13, f32[64,8]{1,0:T(8,128)S(1)} %get-tuple-element.12, pred[64,128]{1,0:T(8,128)(4,1)S(1)} %fusion.30), kind=kOutput, calls=%fused_computation.19 | convolution fusion | flops 50462720 | bytes 1482752 | tf_op jit(solution)/shard_map/pkgt,ptkr->pkgr/dot_general | solution.py:90
  34.8 0.2 fusion.19
  35.1 0.4 copy.74
  35.5 0.4 copy.75
  35.9 0.2 fusion.32
  36.2 1.1 %pad_maximum_fusion = f32[32,2,1,8,130]{4,3,2,1,0:T(8,128)} fusion(f32[32,2,1,8,128]{4,3,2,1,0:T(8,128)S(1)} %bitcast.122, f32[32,2,1,8,1]{4,3,2,1,0:T(8,128)S(1)} %copy.75, f32[32,2,1,8,1]{4,3,2,1,0:T(8,128)S(1)} %copy.74), kind=kLoop, calls=%fused_computation.22 | loop fusion | flops 133120 | bytes 532480 | tf_op jit(solution)/shard_map/concatenate | solution.py:29
  37.3 5.3 %all-to-all-start.1 = ((f32[32,2,1,8,130]{4,3,2,1,0:T(8,128)}), f32[32,2,1,8,130]{4,3,2,1,0:T(8,128)S(1)}, u32[]{:S(2)}, u32[]{:S(2)}) async-start(f32[32,2,1,8,130]{4,3,2,1,0:T(8,128)} %pad_maximum_fusion), calls=%async_computation.1 | async-start | bytes 1048576 | tf_op jit(solution)/shard_map/all_to_all | solution.py:31
  43.0 0.5 fusion.11
  43.4 14.4 %all-to-all-done.1 = f32[32,2,1,8,130]{4,3,2,1,0:T(8,128)S(1)} async-done(((f32[32,2,1,8,130]{4,3,2,1,0:T(8,128)}), f32[32,2,1,8,130]{4,3,2,1,0:T(8,128)S(1)}, u32[]{:S(2)}, u32[]{:S(2)}) %all-to-all-start.1) | async-done | bytes 266272 | tf_op jit(solution)/shard_map/all_to_all | solution.py:31
  57.8 0.4 slice_reduce_fusion
  58.3 0.2 fusion.9
  58.6 0.1 slice.35
  58.8 0.3 fusion.18
  59.2 0.2 fusion.7
  59.4 21.3 %all_to_all.20 = bf16[32,8,1024]{2,1,0:T(8,128)(2,1)S(1)} all-to-all(bf16[32,8,1024]{2,1,0:T(8,128)(2,1)S(1)} %broadcast_in_dim.133), channel_id=1, replica_groups=mesh['dp'=32,'mp'=8] {'dp'}, dimensions={0} | all-to-all | bytes 1048576 | tf_op jit(solution)/shard_map/all_to_all | solution.py:13
  80.7 0.3 fusion.14
  81.0 14.2 %all_to_all.21 = f32[8,32,256]{2,1,0:T(8,128)S(1)} all-to-all(f32[8,32,256]{2,1,0:T(8,128)S(1)} %fusion.14), channel_id=1, replica_groups=mesh['dp'=32,'mp'=8] {'mp'}, dimensions={0} | all-to-all | bytes 524288 | tf_op jit(solution)/shard_map/all_to_all | solution.py:50
  95.2 0.6 reduce_sum.59
  (60 shorter events, 3.2 us)
Async XLA Ops:
  0.0 80.7 %copy-start = (bf16[1024,256]{1,0:T(8,128)(2,1)S(1)}, bf16[1024,256]{1,0:T(8,128)(2,1)}, u32[]{:S(2)}) copy-start(bf16[1024,256]{1,0:T(8,128)(2,1)} %param.15) | copy-start | bytes 1572868
  0.0 17.2 %copy-start.3 = (bf16[8,8,128]{2,1,0:T(8,128)(2,1)S(1)}, bf16[8,8,128]{2,1,0:T(8,128)(2,1)}, u32[]{:S(2)}) copy-start(bf16[8,8,128]{2,1,0:T(8,128)(2,1)} %param.8) | copy-start | bytes 49156
  0.0 18.4 %copy-start.1 = (s32[256]{0:T(256)S(1)}, s32[256]{0:T(256)}, u32[]{:S(2)}) copy-start(s32[256]{0:T(256)} %param.13) | copy-start | bytes 3076
  0.0 17.2 %copy-start.4 = (bf16[1,64,128]{2,1,0:T(8,128)(2,1)S(1)}, bf16[1,64,128]{2,1,0:T(8,128)(2,1)}, u32[]{:S(2)}) copy-start(bf16[1,64,128]{2,1,0:T(8,128)(2,1)} %param.11) | copy-start | bytes 49156
  1.7 28.4 %all-to-all-start = ((bf16[32,8,8,128]{3,2,1,0:T(8,128)(2,1)}), bf16[32,8,8,128]{3,2,1,0:T(8,128)(2,1)}, u32[]{:S(2)}, u32[]{:S(2)}) async-start(bf16[32,8,8,128]{3,2,1,0:T(8,128)(2,1)} %broadcast_in_dim.126), calls=%async_computation | async-start | bytes 1048576 | tf_op jit(solution)/shard_map/all_to_all | solution.py:13
  19.7 3.3 %copy-start.2 = (bf16[8,256,1,128]{3,1,2,0:T(8,128)(2,1)S(1)}, bf16[8,256,1,128]{3,1,2,0:T(8,128)(2,1)}, u32[]{:S(2)}) copy-start(bf16[8,256,1,128]{3,1,2,0:T(8,128)(2,1)} %param.9) | copy-start | bytes 1572868
  32.0 3.9 %copy-start.5 = (bf16[1,64,128]{2,1,0:T(8,128)(2,1)S(1)}, bf16[1,64,128]{2,1,0:T(8,128)(2,1)}, u32[]{:S(2)}) copy-start(bf16[1,64,128]{2,1,0:T(8,128)(2,1)} %param.12) | copy-start | bytes 49156
  37.3 20.5 %all-to-all-start.1 = ((f32[32,2,1,8,130]{4,3,2,1,0:T(8,128)}), f32[32,2,1,8,130]{4,3,2,1,0:T(8,128)S(1)}, u32[]{:S(2)}, u32[]{:S(2)}) async-start(f32[32,2,1,8,130]{4,3,2,1,0:T(8,128)} %pad_maximum_fusion), calls=%async_computation.1 | async-start | bytes 1048576 | tf_op jit(solution)/shard_map/all_to_all | solution.py:31
where the time goes:
time: 96.4 us; the launch traced here: 95.8 us
  blocking collectives  35.5 us (37%)
  waiting for transfers between devices  20.7 us (21%)
  starting transfers between devices  17.4 us (18%)
  local copies, waits for them, and re-layouts  12.6 us (13%)
  matrix products  5.44 us (6%)
  other arithmetic  3.89 us (4%)
    all_to_all x1, blocking collectives, copy_for_each(): lax.all_to_all(jnp.broadcast_to(x[None], (peers, *x.shape)), axis, 0, 0,...  21.3 us
    all_to_all x1, waiting for transfers between devices, sent_together(): lax.all_to_all(both, axis, split_axis=split_dim, concat_axis=concat_dim,...  14.4 us
    all_to_all x1, blocking collectives, sum_at_owner(): tiles = lax.all_to_all(split_up(x, dim, peers), axis, 0, 0, tiled=True)  14.2 us
    all_to_all x1, starting transfers between devices, copy_for_each(): lax.all_to_all(jnp.broadcast_to(x[None], (peers, *x.shape)), axis, 0, 0,...  12.2 us
    all_to_all x1, waiting for transfers between devices, copy_for_each(): lax.all_to_all(jnp.broadcast_to(x[None], (peers, *x.shape)), axis, 0, 0,...  6.3 us
    all_to_all x1, starting transfers between devices, sent_together(): lax.all_to_all(both, axis, split_axis=split_dim, concat_axis=concat_dim,...  5.25 us
    unnamed x15, local copies, waits for them, and re-layouts  4.14 us
    dot_general x2, matrix products, page_partials(): jnp.einsum('pkgt,ptkr->pkgr', weights, latent_vector[..., key_width:].ast...  2.26 us
  transfers between devices with their start and end apart: 2, of which 2 were waited for; matrix products, arithmetic and copies ran while one was open for 11% of the time, Pallas kernels for 0%

commit v1 on v0

v1 whole, which is shorter than its diff:
```python
import functools
import math

import jax
import jax.numpy as jnp
from jax import lax
from jax.experimental import pallas as pl
from jax.experimental.pallas import tpu as pltpu
from jax.sharding import PartitionSpec as P

MESH = pl.DeviceIdType.MESH
very_low = -1e30
f32, bf16, i32 = jnp.float32, jnp.bfloat16, jnp.int32

SEQS = 8
HEADS = 8
SLOTS = 2
PAGE = 128
LANES = 128
RANK = 64


def iota(shape, dim):
    return lax.broadcasted_iota(i32, shape, dim)


def ones_where(condition, kind=bf16):
    return jnp.where(condition, 1.0, 0.0).astype(kind)


def dot(a, b):
    return jnp.dot(a, b, preferred_element_type=f32)


def dot_last(a, b):
    return lax.dot_general(a, b, (((1,), (1,)), ((), ())), preferred_element_type=f32)


def dot_first(a, b):
    return lax.dot_general(a, b, (((0,), (0,)), ((), ())), preferred_element_type=f32)


def rounded(x):
    return x.astype(bf16).astype(f32)


def three_pieces(x):
    top = rounded(x)
    middle = rounded(x - top)
    return top, middle, (x - top) - middle


def distance_order(nz):
    return sorted(range(nz), key=lambda dz: (min(dz, nz - dz), dz))


def kernel(
    nz,
    ny,
    nm,
    scale,
    q_ref,
    res_ref,
    ovf_ref,
    wk_ref,
    wv_ref,
    len_ref,
    rt_ref,
    w_ref,
    out_ref,
    pages,
    resident,
    wbuf,
    w_top,
    w_low,
    chosen,
    counts,
    q_send,
    q_recv,
    p_send,
    p_recv,
    own_lat,
    all_lat,
    own_part,
    r_send,
    r_recv,
    page_sem,
    local_sem,
    qs_sem,
    qr_sem,
    ps_sem,
    pr_sem,
    as_sem,
    ar_sem,
    rs_sem,
    rr_sem,
):
    me, mp = lax.axis_index("dp"), lax.axis_index("mp")
    z, y = lax.div(me, ny), lax.rem(me, ny)
    groups = nz * ny
    items = groups * SLOTS
    rows = items * HEADS
    tail = rt_ref.shape[0]
    total = groups * SEQS
    home_tokens = resident.shape[1]

    def group_at(dz, dy):
        return lax.rem(z + dz, nz) * ny + lax.rem(y + dy, ny)

    def holder_at(dz, ya):
        return lax.rem(z + dz, nz) * ny + ya

    def source_at(dz, ya):
        return lax.rem(z + nz - dz, nz) * ny + ya

    def others_in_plane(dz):
        return [lax.rem(y + dy, ny) for dy in range(1 if dz == 0 else 0, ny)]

    barrier = pltpu.get_barrier_semaphore()

    def greet_group(step, carry):
        peer = group_at(lax.div(step, ny), lax.rem(step, ny))
        pl.semaphore_signal(barrier, inc=1, device_id=(peer, mp), device_id_type=MESH)
        return carry

    def greet_member(step, carry):
        peer = lax.rem(mp + step, nm)
        pl.semaphore_signal(barrier, inc=1, device_id=(me, peer), device_id_type=MESH)
        return carry

    lax.fori_loop(1, groups, greet_group, 0)
    lax.fori_loop(1, nm, greet_member, 0)

    near_first = distance_order(nz)
    far_first = near_first[::-1]

    resident_copy = pltpu.make_async_copy(res_ref, resident, local_sem.at[0])
    resident_copy.start()
    page_copies = {}
    for dz in near_first:
        first = lax.rem(z + nz - dz, nz) * ny
        page_copies[dz] = pltpu.make_async_copy(
            ovf_ref.at[pl.ds(first, ny)], pages.at[pl.ds(dz * ny, ny)], page_sem.at[dz]
        )
        page_copies[dz].start()
    weight_copy = pltpu.make_async_copy(w_ref, wbuf, local_sem.at[1])
    weight_copy.start()

    routes = jnp.concatenate([rt_ref[p] for p in range(tail)], axis=0).astype(f32)
    lens = len_ref[...].astype(f32)

    entry = iota((items, LANES), 0)
    lane = iota((items, LANES), 1)
    entry_dz, entry_y, entry_c = entry // (ny * SLOTS), (entry // SLOTS) % ny, entry % SLOTS
    holder = (((z + entry_dz) % nz) * ny + entry_y).astype(f32)
    own_columns = ones_where(
        iota((total, LANES), 0) == me * SEQS + iota((total, LANES), 1) % SEQS
    )
    own_routes = dot(routes.astype(bf16), own_columns)
    named = [jnp.where(own_routes[p : p + 1] == holder, 1.0, 0.0) for p in range(tail)]
    row_l, column_l = iota((LANES, LANES), 0), iota((LANES, LANES), 1)
    earlier = ones_where(
        (row_l // SEQS == column_l // SEQS) & (row_l % SEQS < column_l % SEQS)
    )
    before = dot(functools.reduce(jnp.add, named).astype(bf16), earlier)
    picked = jnp.zeros((items, LANES), f32)
    wanted = entry_c.astype(f32)
    for match in named:
        picked = picked + jnp.where(before == wanted, match, 0.0)
        before = before + match
    expand = ones_where(iota((rows, items), 0) // HEADS == iota((rows, items), 1))
    row = iota((rows, LANES), 0)
    row_lane = iota((rows, LANES), 1)
    same_head = row_lane // SEQS == row % HEADS
    picks = jnp.where(same_head, dot(expand, picked.astype(bf16)), 0.0).astype(bf16)
    chosen[pl.ds(0, rows), :] = picks

    home_row, home_lane = iota((64, LANES), 0), iota((64, LANES), 1)
    turned = ones_where(
        (home_lane // SEQS == home_row % HEADS) & (home_lane % SEQS == home_row // HEADS)
    )
    chosen[pl.ds(rows, 64), :] = turned
    chosen[pl.ds(rows + 64, 64), :] = turned
    queries = q_ref[...]
    by_head = dot_first(turned, queries).astype(bf16)
    q_send[...] = dot(picks, by_head).astype(bf16).reshape(groups, SLOTS * HEADS, LANES)

    sequence = iota((total, total), 0)
    later = iota((total, total), 1)
    held_before = ones_where((sequence // SEQS == later // SEQS) & (sequence < later))
    here = jnp.where(routes == me.astype(f32), 1.0, 0.0)
    rank = dot(jnp.sum(here, axis=0, keepdims=True).astype(bf16), held_before)
    room = [jnp.zeros((1, total), f32) for _ in range(SLOTS)]
    for p in range(tail):
        match = here[p : p + 1]
        valid = jnp.clip(lens - (home_tokens + p * PAGE), 0.0, float(PAGE)) * match
        for c in range(SLOTS):
            room[c] = room[c] + jnp.where(rank == float(c), valid, 0.0)
        rank = rank + match
    entry_s = iota((items, total), 0)
    column_s = iota((items, total), 1)
    source = ((z + nz - entry_s // (ny * SLOTS)) % nz) * ny + (entry_s // SLOTS) % ny
    sized = jnp.where(entry_s % SLOTS == 0, room[0], room[1])
    sized = jnp.where(column_s // SEQS == source, sized, 0.0).astype(bf16)
    all_ones = jnp.ones((total, LANES), bf16)
    per_item = dot(sized, all_ones).astype(bf16)
    counts[...] = dot(expand, per_item)

    home_s = iota((64, total), 1) == me * SEQS + iota((64, total), 0) // HEADS
    home_count = dot(
        jnp.where(home_s, jnp.minimum(lens, float(home_tokens)), 0.0).astype(bf16), all_ones
    )

    pl.semaphore_wait(barrier, groups - 1 + nm - 1)

    def query_copy(dz, ya_source_slot, ya_target_slot, peer):
        return pltpu.make_async_remote_copy(
            src_ref=q_send.at[dz * ny + ya_source_slot],
            dst_ref=q_recv.at[dz * ny + ya_target_slot],
            send_sem=qs_sem.at[dz * ny + ya_source_slot],
            recv_sem=qr_sem.at[dz * ny + ya_target_slot],
            device_id=(peer, mp),
            device_id_type=MESH,
        )

    def part_copy(dz, ya_source_slot, ya_target_slot, peer):
        return pltpu.make_async_remote_copy(
            src_ref=p_send.at[dz * ny + ya_source_slot],
            dst_ref=p_recv.at[dz * ny + ya_target_slot],
            send_sem=ps_sem.at[dz * ny + ya_source_slot],
            recv_sem=pr_sem.at[dz * ny + ya_target_slot],
            device_id=(peer, mp),
            device_id_type=MESH,
        )

    for dz in far_first:
        for ya in others_in_plane(dz):
            query_copy(dz, ya, y, holder_at(dz, ya)).start()
    q_recv[y] = q_send[y]

    wk_wide = jnp.concatenate([wk_ref[...], jnp.zeros((RANK, LANES), bf16)], axis=0)

    def message(best, sums, mixed):
        at = iota(mixed.shape, 1)
        best_pieces, sum_pieces = three_pieces(best), three_pieces(sums)
        packed = mixed
        for i in range(3):
            packed = jnp.where(at == i, best_pieces[i], packed)
            packed = jnp.where(at == 3 + i, sum_pieces[i], packed)
        return packed, at

    def partials(query_rows, latents, token_count):
        folded = three_pieces(dot_last(query_rows, wk_wide))
        scores = []
        for i, latent in enumerate(latents):
            stacked = jnp.concatenate([f[8 * i : 8 * i + 8] for f in folded], axis=0)
            s = dot_last(stacked.astype(bf16), latent)
            scores.append(s[0:8] + s[8:16] + s[16:24])
        scores = jnp.concatenate(scores, axis=0) * scale
        mask = iota(scores.shape, 1).astype(f32) < token_count
        scores = jnp.where(mask, scores, very_low)
        best = jnp.max(scores, axis=1, keepdims=True)
        weights = jnp.where(mask, jnp.exp(scores - best), 0.0)
        sums = jnp.sum(weights, axis=1, keepdims=True)
        top = rounded(weights)
        low = weights - top
        mixed = []
        for i, latent in enumerate(latents):
            stacked = jnp.concatenate([top[8 * i : 8 * i + 8], low[8 * i : 8 * i + 8]], axis=0)
            o = dot(stacked.astype(bf16), latent)
            mixed.append(o[0:8] + o[8:16])
        return best, sums, jnp.concatenate(mixed, axis=0)

    resident_copy.wait()
    wide_count = jnp.concatenate([home_count] * (home_tokens // LANES), axis=1)
    best, sums, mixed = partials(queries, [resident[k] for k in range(SEQS)], wide_count)
    packed, at = message(best, sums, mixed)
    p_recv[pl.ds(groups, 4)] = packed.astype(bf16).reshape(4, 16, LANES)
    remainder = jnp.where((at >= 3) & (at < RANK), 0.0, packed - rounded(packed))
    remainder = jnp.where(at < 3, packed, remainder)
    p_recv[pl.ds(groups + 4, 4)] = remainder.astype(bf16).reshape(4, 16, LANES)

    weight_copy.wait()
    for h in range(HEADS):
        joined = dot(wv_ref[...], wbuf[pl.ds(h * LANES, LANES), :])
        w_top[pl.ds(h * RANK, RANK), :] = joined.astype(bf16)
        w_low[pl.ds(h * RANK, RANK), :] = (joined - rounded(joined)).astype(bf16)

    for dz in near_first:
        page_copies[dz].wait()
        for ya in others_in_plane(dz):
            query_copy(dz, ya, ya, holder_at(dz, ya)).wait_recv()
        block = q_recv[pl.ds(dz * ny, ny)].reshape(ny * SLOTS * HEADS, LANES)
        latents = [
            pages[dz * ny + i // SLOTS, pl.ds((i % SLOTS) * PAGE, PAGE), :]
            for i in range(ny * SLOTS)
        ]
        chunk = ny * SLOTS * HEADS
        best, sums, mixed = partials(block, latents, counts[pl.ds(dz * chunk, chunk), :])
        packed, _ = message(best, sums, mixed)
        p_send[pl.ds(dz * ny, ny)] = packed.astype(bf16).reshape(ny, SLOTS * HEADS, LANES)
        for ya in others_in_plane(dz):
            part_copy(dz, ya, y, source_at(dz, ya)).start()
        if dz == 0:
            p_recv[y] = p_send[y]

    for dz in near_first:
        for ya in others_in_plane(dz):
            part_copy(dz, ya, ya, source_at(dz, ya)).wait_recv()
    parts = p_recv[...].reshape(rows + 128, LANES)
    peaks = dot(parts, ones_where(iota((LANES, LANES), 0) < 3))
    member = chosen[...].astype(f32) > 0.5
    peak = jnp.max(jnp.where(member, peaks, very_low), axis=0, keepdims=True)
    factor = jnp.where(member, jnp.exp(peaks - peak), 0.0)
    factor_top = factor.astype(bf16)
    factor_low = (factor - factor_top.astype(f32)).astype(bf16)
    merged = (dot_first(factor_top, parts) + dot_first(factor_low, parts))[0:64]
    merged_sum = merged[:, 3:4] + merged[:, 4:5] + merged[:, 5:6]
    latent = merged / merged_sum
    low_lane = iota((SEQS, LANES), 1) < RANK
    for v in range(HEADS // 2):
        even = latent[16 * v : 16 * v + 8]
        odd = latent[16 * v + 8 : 16 * v + 16]
        own_lat[:, pl.ds(v * LANES, LANES)] = jnp.where(
            low_lane, pltpu.roll(even, RANK, 1), odd
        ).astype(bf16)

    def latent_copy(dz, ya, slot, peer):
        return pltpu.make_async_remote_copy(
            src_ref=own_lat,
            dst_ref=all_lat.at[slot],
            send_sem=as_sem.at[dz * ny + ya],
            recv_sem=ar_sem.at[slot],
            device_id=(peer, mp),
            device_id_type=MESH,
        )

    for dz in far_first:
        for ya in others_in_plane(dz):
            latent_copy(dz, ya, me, holder_at(dz, ya)).start()
    all_lat[me] = own_lat[...]

    def sum_copy(target):
        slot = lax.rem(mp + nm - target, nm)
        return pltpu.make_async_remote_copy(
            src_ref=r_send.at[target],
            dst_ref=r_recv.at[slot],
            send_sem=rs_sem.at[target],
            recv_sem=rr_sem.at[slot],
            device_id=(me, target),
            device_id_type=MESH,
        )

    for dz in near_first:
        target = lax.rem(z + nz - dz, nz)
        for ya in others_in_plane(dz):
            source_group = source_at(dz, ya)
            latent_copy(dz, ya, source_group, source_group).wait_recv()
        block = all_lat[pl.ds(target * ny, ny)].reshape(ny * SEQS, HEADS * RANK)
        part = dot(block, w_top[...]) + dot(block, w_low[...])

        @pl.when(target == mp)
        def _():
            own_part[...] = part

        @pl.when(target != mp)
        def _():
            r_send[target] = part.astype(bf16)
            sum_copy(target).start()

    summed = own_part[...]
    for step in range(1, nm):
        pltpu.make_async_remote_copy(
            src_ref=r_send.at[lax.rem(mp + step, nm)],
            dst_ref=r_recv.at[step],
            send_sem=rs_sem.at[lax.rem(mp + step, nm)],
            recv_sem=rr_sem.at[step],
            device_id=(me, lax.rem(mp + step, nm)),
            device_id_type=MESH,
        ).wait_recv()
        summed = summed + r_recv[step].astype(f32)
    out_ref[...] = summed.astype(bf16)

    for dz in range(nz):
        for ya in others_in_plane(dz):
            query_copy(dz, ya, y, holder_at(dz, ya)).wait_send()
            part_copy(dz, ya, y, source_at(dz, ya)).wait_send()
            latent_copy(dz, ya, me, holder_at(dz, ya)).wait_send()
    for step in range(1, nm):
        sum_copy(lax.rem(mp + step, nm)).wait_send()


def body(
    nz,
    ny,
    queries,
    resident_cache,
    overflow_cache,
    key_up_weight,
    value_up_weight,
    lengths,
    routes,
    out_weight,
):
    nm = lax.axis_size("mp")
    groups = nz * ny
    home_tokens = resident_cache.shape[1]
    out_columns = out_weight.shape[1]
    total = lengths.shape[0]
    tail = routes.shape[1]
    rows = groups * SLOTS * HEADS
    args = (
        queries.reshape(SEQS * HEADS, LANES),
        resident_cache.reshape(SEQS, home_tokens, LANES),
        overflow_cache.reshape(groups, SLOTS * PAGE, LANES),
        key_up_weight.reshape(RANK, LANES),
        value_up_weight.reshape(RANK, LANES),
        lengths.reshape(1, total),
        routes.transpose(1, 2, 0),
        out_weight,
    )
    in_vmem = pl.BlockSpec(memory_space=pltpu.VMEM)
    anywhere = pl.BlockSpec(memory_space=pl.ANY)
    dma = pltpu.SemaphoreType.DMA
    return pl.pallas_call(
        functools.partial(kernel, nz, ny, nm, 1.0 / math.sqrt(LANES)),
        out_shape=jax.ShapeDtypeStruct((ny * SEQS, out_columns), bf16),
        in_specs=[in_vmem, anywhere, anywhere, in_vmem, in_vmem, in_vmem, in_vmem, anywhere],
        out_specs=in_vmem,
        scratch_shapes=[
            pltpu.VMEM((groups, SLOTS * PAGE, LANES), bf16),
            pltpu.VMEM((SEQS, home_tokens, LANES), bf16),
            pltpu.VMEM(out_weight.shape, bf16),
            pltpu.VMEM((HEADS * RANK, out_columns), bf16),
            pltpu.VMEM((HEADS * RANK, out_columns), bf16),
            pltpu.VMEM((rows + 128, LANES), bf16),
            pltpu.VMEM((rows, LANES), f32),
            pltpu.VMEM((groups, SLOTS * HEADS, LANES), bf16),
            pltpu.VMEM((groups, SLOTS * HEADS, LANES), bf16),
            pltpu.VMEM((groups, SLOTS * HEADS, LANES), bf16),
            pltpu.VMEM((groups + 8, SLOTS * HEADS, LANES), bf16),
            pltpu.VMEM((SEQS, HEADS * RANK), bf16),
            pltpu.VMEM((groups, SEQS, HEADS * RANK), bf16),
            pltpu.VMEM((ny * SEQS, out_columns), f32),
            pltpu.VMEM((nm, ny * SEQS, out_columns), bf16),
            pltpu.VMEM((nm, ny * SEQS, out_columns), bf16),
            dma((nz,)),
            dma((2,)),
            dma((groups,)),
            dma((groups,)),
            dma((groups,)),
            dma((groups,)),
            dma((groups,)),
            dma((groups,)),
            dma((nm,)),
            dma((nm,)),
        ],
        compiler_params=pltpu.CompilerParams(collective_id=0, has_side_effects=True),
        name="spilled_attention",
    )(*args)


def solution(mesh):
    placed = (
        P("dp", "mp", None),
        P("dp", None, "mp", None),
        P("dp", None, None, None, "mp", None),
        P("mp", None, None),
        P("mp", None, None),
        P(),
        P(),
        P("mp", "dp"),
    )
    nz = mesh.shape["mp"]
    ny = mesh.shape["dp"] // nz
    return jax.shard_map(
        functools.partial(body, nz, ny),
        mesh=mesh,
        in_specs=placed,
        out_specs=P("mp", "dp"),
        check_vma=False,
    )
```

time: 96.4 us -> 43.5 us (0.45)
  Pallas kernels: 0 us -> 41.9 us
  blocking collectives: 35.5 us -> 0 us
  waiting for transfers between devices: 20.7 us -> 0 us
  starting transfers between devices: 17.4 us -> 0 us
  local copies, waits for them, and re-layouts: 12.6 us -> 1.32 us
  matrix products: 5.44 us -> 0 us
  other arithmetic: 3.89 us -> 0 us
    pallas_call x0 -> x1, Pallas kernels: none -> 41.9 us  [body(): pl.pallas_call(functools.partial(kernel, nz, ny, nm, 1.0 / math.sqrt(LANE...]
    all_to_all x2 -> x0, blocking collectives: 35.5 us -> none  [the longest x1 21.3 us: copy_for_each(): lax.all_to_all(jnp.broadcast_to(x[None], (peers, *x.shape)), axis, 0, 0,...]
    all_to_all x2 -> x0, waiting for transfers between devices: 20.7 us -> none  [the longest x1 14.4 us: sent_together(): lax.all_to_all(both, axis, split_axis=split_dim, concat_axis=concat_dim,...]
    all_to_all x2 -> x0, starting transfers between devices: 17.4 us -> none  [the longest x1 12.2 us: copy_for_each(): lax.all_to_all(jnp.broadcast_to(x[None], (peers, *x.shape)), axis, 0, 0,...]
    dot_general x12 -> x0, matrix products: 5.44 us -> none  [the longest x2 2.26 us: page_partials(): jnp.einsum('pkgt,ptkr->pkgr', weights, latent_vector[..., key_width:].ast...]
    unnamed x15 -> x1, local copies, waits for them, and re-layouts: 4.14 us -> 1.32 us
    gather x2 -> x0, local copies, waits for them, and re-layouts: 2.46 us -> none  [the longest x1 1.67 us: body(): all_queries[sequence.reshape(item_count)]]
    reduce_sum x6 -> x0, other arithmetic: 2.12 us -> none  [the longest x1 0.85 us: spill_ranks(): return jnp.sum((same_target & earlier).astype(jnp.int32), axis=-1)]
  transfers between devices with their start and end apart: 2 -> 0, of which waited for: 2 -> 0; matrix products, arithmetic and copies ran while one was open for 11% -> 0% of each run, Pallas kernels for 0% -> 0%
where the time goes in v1:
time: 43.5 us; the launch traced here: 43.2 us
  Pallas kernels  41.9 us (96%)
  local copies, waits for them, and re-layouts  1.32 us (3%)
    pallas_call x1, Pallas kernels, body(): pl.pallas_call(functools.partial(kernel, nz, ny, nm, 1.0 / math.sqrt(LANE...  41.9 us
    unnamed x1, local copies, waits for them, and re-layouts  1.32 us

profile of v1, /device:TPU:1, one launch (start us, length us, event | category | flops | bytes accessed | tf_op | source)
XLA Modules:
  0.0 43.2 jit_solution(12342302072416882962)
XLA Ops:
  0.0 41.9 %spilled_attention.1 = bf16[32,256]{1,0:T(8,128)(2,1)} custom-call(bf16[64,128]{1,0:T(8,128)(2,1)} %bitcast.9, bf16[8,256,128]{2,1,0:T(8,128)(2,1)} %bitcast.8, bf16[32,256,128]{2,1,0:T(8,128)(2,1)} %bitcast.7, bf16[64,128]{1,0:T(8,128)(2,1)} %bitcast.10, bf16[64,128]{1,0:T(8,128)(2,1)} %bitcast.11, s32[1,256]{1,0:T(1,128)} %bitcast.13, ...), custom_call_target="tpu_custom_call" | custom-call | tf_op jit(solution)/shard_map/spilled_attention/pallas_call | solution.py:425
  41.9 1.3 %copy.10 = bf16[32,256]{1,0:T(8,128)(2,1)} copy(bf16[32,256]{1,0:T(8,128)(2,1)} %spilled_attention.1) | data formatting | bytes 32768

commit v2 on v1

--- a/solution.py
+++ b/solution.py
@@ -54,20 +54,34 @@
     return sorted(range(nz), key=lambda dz: (min(dz, nz - dz), dz))
 
 
+def batches(order, sizes):
+    cut, at = [], 0
+    for size in sizes:
+        if order[at : at + size]:
+            cut.append(order[at : at + size])
+        at += size
+    return cut
+
+
 def kernel(
     nz,
     ny,
     nm,
     scale,
-    q_ref,
+    q_hbm,
     res_ref,
     ovf_ref,
+    wk_hbm,
+    wv_hbm,
+    len_hbm,
+    rt_hbm,
+    w_ref,
+    out_ref,
+    q_ref,
     wk_ref,
     wv_ref,
     len_ref,
     rt_ref,
-    w_ref,
-    out_ref,
     pages,
     resident,
     wbuf,
@@ -118,33 +132,51 @@
 
     barrier = pltpu.get_barrier_semaphore()
 
-    def greet_group(step, carry):
-        peer = group_at(lax.div(step, ny), lax.rem(step, ny))
-        pl.semaphore_signal(barrier, inc=1, device_id=(peer, mp), device_id_type=MESH)
-        return carry
-
-    def greet_member(step, carry):
-        peer = lax.rem(mp + step, nm)
-        pl.semaphore_signal(barrier, inc=1, device_id=(me, peer), device_id_type=MESH)
-        return carry
-
-    lax.fori_loop(1, groups, greet_group, 0)
-    lax.fori_loop(1, nm, greet_member, 0)
-
     near_first = distance_order(nz)
     far_first = near_first[::-1]
-
-    resident_copy = pltpu.make_async_copy(res_ref, resident, local_sem.at[0])
-    resident_copy.start()
-    page_copies = {}
-    for dz in near_first:
-        first = lax.rem(z + nz - dz, nz) * ny
-        page_copies[dz] = pltpu.make_async_copy(
-            ovf_ref.at[pl.ds(first, ny)], pages.at[pl.ds(dz * ny, ny)], page_sem.at[dz]
-        )
-        page_copies[dz].start()
-    weight_copy = pltpu.make_async_copy(w_ref, wbuf, local_sem.at[1])
-    weight_copy.start()
+    serve_batches = [[0]] + batches([dz for dz in far_first if dz], (2, 2, 3))
+    project_batches = [[0]] + batches([dz for dz in near_first if dz], (3, 4))
+
+    def batch_of(dz, cut):
+        return next(i for i, batch in enumerate(cut) if dz in batch)
+
+    def slots_in(batch):
+        return sum(ny - (dz == 0) for dz in batch)
+
+    for dz in far_first:
+        for ya in others_in_plane(dz):
+            pl.semaphore_signal(
+                barrier, inc=1, device_id=(holder_at(dz, ya), mp), device_id_type=MESH
+            )
+    for step in range(1, nm):
+        pl.semaphore_signal(
+            barrier, inc=1, device_id=(me, lax.rem(mp + step, nm)), device_id_type=MESH
+        )
+
+    small = [
+        pltpu.make_async_copy(source, target, local_sem.at[i])
+        for i, (source, target) in enumerate(
+            [
+                (rt_hbm, rt_ref),
+                (len_hbm, len_ref),
+                (q_hbm, q_ref),
+                (wk_hbm, wk_ref),
+                (wv_hbm, wv_ref),
+                (res_ref, resident),
+                (w_ref, wbuf),
+            ]
+        )
+    ]
+    for copy in small:
+        copy.start()
+    for i, batch in enumerate(serve_batches):
+        for dz in batch:
+            first = lax.rem(z + nz - dz, nz) * ny
+            pltpu.make_async_copy(
+                ovf_ref.at[pl.ds(first, ny)], pages.at[pl.ds(dz * ny, ny)], page_sem.at[i]
+            ).start()
+    for copy in small[:5]:
+        copy.wait()
 
     routes = jnp.concatenate([rt_ref[p] for p in range(tail)], axis=0).astype(f32)
     lens = len_ref[...].astype(f32)
@@ -213,29 +245,39 @@
 
     pl.semaphore_wait(barrier, groups - 1 + nm - 1)
 
-    def query_copy(dz, ya_source_slot, ya_target_slot, peer):
+    def query_copy(dz, ya, peer):
         return pltpu.make_async_remote_copy(
-            src_ref=q_send.at[dz * ny + ya_source_slot],
-            dst_ref=q_recv.at[dz * ny + ya_target_slot],
-            send_sem=qs_sem.at[dz * ny + ya_source_slot],
-            recv_sem=qr_sem.at[dz * ny + ya_target_slot],
+            src_ref=q_send.at[dz * ny + ya],
+            dst_ref=q_recv.at[dz * ny + y],
+            send_sem=qs_sem.at[0],
+            recv_sem=qr_sem.at[batch_of(dz, serve_batches)],
             device_id=(peer, mp),
             device_id_type=MESH,
         )
 
-    def part_copy(dz, ya_source_slot, ya_target_slot, peer):
+    def part_copy(dz, ya, peer):
         return pltpu.make_async_remote_copy(
-            src_ref=p_send.at[dz * ny + ya_source_slot],
-            dst_ref=p_recv.at[dz * ny + ya_target_slot],
-            send_sem=ps_sem.at[dz * ny + ya_source_slot],
-            recv_sem=pr_sem.at[dz * ny + ya_target_slot],
+            src_ref=p_send.at[dz * ny + ya],
+            dst_ref=p_recv.at[dz * ny + y],
+            send_sem=ps_sem.at[0],
+            recv_sem=pr_sem.at[0],
             device_id=(peer, mp),
             device_id_type=MESH,
         )
 
+    def many(source, target, count, send_sem, recv_sem):
+        return pltpu.make_async_remote_copy(
+            src_ref=source.at[pl.ds(0, count)],
+            dst_ref=target.at[pl.ds(0, count)],
+            send_sem=send_sem,
+            recv_sem=recv_sem,
+            device_id=(me, mp),
+            device_id_type=MESH,
+        )
+
     for dz in far_first:
         for ya in others_in_plane(dz):
-            query_copy(dz, ya, y, holder_at(dz, ya)).start()
+            query_copy(dz, ya, holder_at(dz, ya)).start()
     q_recv[y] = q_send[y]
 
     wk_wide = jnp.concatenate([wk_ref[...], jnp.zeros((RANK, LANES), bf16)], axis=0)
@@ -271,7 +313,7 @@
             mixed.append(o[0:8] + o[8:16])
         return best, sums, jnp.concatenate(mixed, axis=0)
 
-    resident_copy.wait()
+    small[5].wait()
     wide_count = jnp.concatenate([home_count] * (home_tokens // LANES), axis=1)
     best, sums, mixed = partials(queries, [resident[k] for k in range(SEQS)], wide_count)
     packed, at = message(best, sums, mixed)
@@ -280,33 +322,42 @@
     remainder = jnp.where(at < 3, packed, remainder)
     p_recv[pl.ds(groups + 4, 4)] = remainder.astype(bf16).reshape(4, 16, LANES)
 
-    weight_copy.wait()
+    small[6].wait()
     for h in range(HEADS):
         joined = dot(wv_ref[...], wbuf[pl.ds(h * LANES, LANES), :])
         w_top[pl.ds(h * RANK, RANK), :] = joined.astype(bf16)
         w_low[pl.ds(h * RANK, RANK), :] = (joined - rounded(joined)).astype(bf16)
 
-    for dz in near_first:
-        page_copies[dz].wait()
-        for ya in others_in_plane(dz):
-            query_copy(dz, ya, ya, holder_at(dz, ya)).wait_recv()
-        block = q_recv[pl.ds(dz * ny, ny)].reshape(ny * SLOTS * HEADS, LANES)
+    chunk = ny * SLOTS * HEADS
+    for i, batch in enumerate(serve_batches):
+        held = len(batch) * ny
+        pltpu.make_async_copy(
+            ovf_ref.at[pl.ds(0, held)], pages.at[pl.ds(0, held)], page_sem.at[i]
+        ).wait()
+        many(q_send, q_recv, slots_in(batch), qs_sem.at[0], qr_sem.at[i]).wait_recv()
+        block = jnp.concatenate(
+            [q_recv[pl.ds(dz * ny, ny)].reshape(chunk, LANES) for dz in batch], axis=0
+        )
+        token_count = jnp.concatenate(
+            [counts[pl.ds(dz * chunk, chunk), :] for dz in batch], axis=0
+        )
         latents = [
             pages[dz * ny + i // SLOTS, pl.ds((i % SLOTS) * PAGE, PAGE), :]
+            for dz in batch
             for i in range(ny * SLOTS)
         ]
-        chunk = ny * SLOTS * HEADS
-        best, sums, mixed = partials(block, latents, counts[pl.ds(dz * chunk, chunk), :])
+        best, sums, mixed = partials(block, latents, token_count)
         packed, _ = message(best, sums, mixed)
-        p_send[pl.ds(dz * ny, ny)] = packed.astype(bf16).reshape(ny, SLOTS * HEADS, LANES)
-        for ya in others_in_plane(dz):
-            part_copy(dz, ya, y, source_at(dz, ya)).start()
-        if dz == 0:
-            p_recv[y] = p_send[y]
-
-    for dz in near_first:
-        for ya in others_in_plane(dz):
-            part_copy(dz, ya, ya, source_at(dz, ya)).wait_recv()
+        packed = packed.astype(bf16).reshape(len(batch) * ny, SLOTS * HEADS, LANES)
+        for n, dz in enumerate(batch):
+            p_send[pl.ds(dz * ny, ny)] = packed[n * ny : (n + 1) * ny]
+        for dz in batch:
+            for ya in others_in_plane(dz):
+                part_copy(dz, ya, source_at(dz, ya)).start()
+            if dz == 0:
+                p_recv[y] = p_send[y]
+
+    many(p_send, p_recv, groups - 1, ps_sem.at[0], pr_sem.at[0]).wait_recv()
     parts = p_recv[...].reshape(rows + 128, LANES)
     peaks = dot(parts, ones_where(iota((LANES, LANES), 0) < 3))
     member = chosen[...].astype(f32) > 0.5
@@ -325,69 +376,65 @@
             low_lane, pltpu.roll(even, RANK, 1), odd
         ).astype(bf16)
 
-    def latent_copy(dz, ya, slot, peer):
+    def latent_copy(dz, peer):
         return pltpu.make_async_remote_copy(
             src_ref=own_lat,
-            dst_ref=all_lat.at[slot],
-            send_sem=as_sem.at[dz * ny + ya],
-            recv_sem=ar_sem.at[slot],
+            dst_ref=all_lat.at[me],
+            send_sem=as_sem.at[0],
+            recv_sem=ar_sem.at[batch_of(dz, project_batches)],
             device_id=(peer, mp),
             device_id_type=MESH,
         )
 
     for dz in far_first:
         for ya in others_in_plane(dz):
-            latent_copy(dz, ya, me, holder_at(dz, ya)).start()
+            latent_copy(dz, holder_at(dz, ya)).start()
     all_lat[me] = own_lat[...]
 
     def sum_copy(target):
-        slot = lax.rem(mp + nm - target, nm)
         return pltpu.make_async_remote_copy(
             src_ref=r_send.at[target],
-            dst_ref=r_recv.at[slot],
-            send_sem=rs_sem.at[target],
-            recv_sem=rr_sem.at[slot],
+            dst_ref=r_recv.at[lax.rem(mp + nm - target, nm)],
+            send_sem=rs_sem.at[0],
+            recv_sem=rr_sem.at[0],
             device_id=(me, target),
             device_id_type=MESH,
         )
 
-    for dz in near_first:
-        target = lax.rem(z + nz - dz, nz)
-        for ya in others_in_plane(dz):
-            source_group = source_at(dz, ya)
-            latent_copy(dz, ya, source_group, source_group).wait_recv()
-        block = all_lat[pl.ds(target * ny, ny)].reshape(ny * SEQS, HEADS * RANK)
+    for i, batch in enumerate(project_batches):
+        many(all_lat, all_lat, slots_in(batch), as_sem.at[0], ar_sem.at[i]).wait_recv()
+        block = jnp.concatenate(
+            [
+                all_lat[pl.ds(lax.rem(z + nz - dz, nz) * ny, ny)].reshape(
+                    ny * SEQS, HEADS * RANK
+                )
+                for dz in batch
+            ],
+            axis=0,
+        )
         part = dot(block, w_top[...]) + dot(block, w_low[...])
-
-        @pl.when(target == mp)
-        def _():
-            own_part[...] = part
-
-        @pl.when(target != mp)
-        def _():
-            r_send[target] = part.astype(bf16)
-            sum_copy(target).start()
-
+        for n, dz in enumerate(batch):
+            target = lax.rem(z + nz - dz, nz)
+            piece = part[n * ny * SEQS : (n + 1) * ny * SEQS]
+
+            @pl.when(target == mp)
+            def _():
+                own_part[...] = piece
+
+            @pl.when(target != mp)
+            def _():
+                r_send[target] = piece.astype(bf16)
+                sum_copy(target).start()
+
+    many(r_send, r_recv, nm - 1, rs_sem.at[0], rr_sem.at[0]).wait_recv()
     summed = own_part[...]
     for step in range(1, nm):
-        pltpu.make_async_remote_copy(
-            src_ref=r_send.at[lax.rem(mp + step, nm)],
-            dst_ref=r_recv.at[step],
-            send_sem=rs_sem.at[lax.rem(mp + step, nm)],
-            recv_sem=rr_sem.at[step],
-            device_id=(me, lax.rem(mp + step, nm)),
-            device_id_type=MESH,
-        ).wait_recv()
         summed = summed + r_recv[step].astype(f32)
     out_ref[...] = summed.astype(bf16)
-
-    for dz in range(nz):
-        for ya in others_in_plane(dz):
-            query_copy(dz, ya, y, holder_at(dz, ya)).wait_send()
-            part_copy(dz, ya, y, source_at(dz, ya)).wait_send()
-            latent_copy(dz, ya, me, holder_at(dz, ya)).wait_send()
-    for step in range(1, nm):
-        sum_copy(lax.rem(mp + step, nm)).wait_send()
+    many(q_send, q_recv, groups - 1, qs_sem.at[0], qr_sem.at[0]).wait_send()
+    many(p_send, p_recv, groups - 1, ps_sem.at[0], pr_sem.at[0]).wait_send()
+    many(all_lat, all_lat, groups - 1, as_sem.at[0], ar_sem.at[0]).wait_send()
+    many(r_send, r_recv, nm - 1, rs_sem.at[0], rr_sem.at[0]).wait_send()
 
 
 def body(
@@ -425,9 +472,14 @@
     return pl.pallas_call(
         functools.partial(kernel, nz, ny, nm, 1.0 / math.sqrt(LANES)),
         out_shape=jax.ShapeDtypeStruct((ny * SEQS, out_columns), bf16),
-        in_specs=[in_vmem, anywhere, anywhere, in_vmem, in_vmem, in_vmem, in_vmem, anywhere],
+        in_specs=[anywhere] * 8,
         out_specs=in_vmem,
         scratch_shapes=[
+            pltpu.VMEM((SEQS * HEADS, LANES), bf16),
+            pltpu.VMEM((RANK, LANES), bf16),
+            pltpu.VMEM((RANK, LANES), bf16),
+            pltpu.VMEM((1, total), i32),
+            pltpu.VMEM((tail, 1, total), i32),
             pltpu.VMEM((groups, SLOTS * PAGE, LANES), bf16),
             pltpu.VMEM((SEQS, home_tokens, LANES), bf16),
             pltpu.VMEM(out_weight.shape, bf16),
@@ -444,16 +496,16 @@
             pltpu.VMEM((ny * SEQS, out_columns), f32),
             pltpu.VMEM((nm, ny * SEQS, out_columns), bf16),
             pltpu.VMEM((nm, ny * SEQS, out_columns), bf16),
-            dma((nz,)),
-            dma((2,)),
-            dma((groups,)),
-            dma((groups,)),
-            dma((groups,)),
-            dma((groups,)),
-            dma((groups,)),
-            dma((groups,)),
-            dma((nm,)),
-            dma((nm,)),
+            dma((4,)),
+            dma((7,)),
+            dma((1,)),
+            dma((4,)),
+            dma((1,)),
+            dma((1,)),
+            dma((1,)),
+            dma((3,)),
+            dma((1,)),
+            dma((1,)),
         ],
         compiler_params=pltpu.CompilerParams(collective_id=0, has_side_effects=True),
         name="spilled_attention",

time: 43.5 us -> 39.1 us (0.90)
  Pallas kernels: 41.9 us -> 37.6 us
    pallas_call x1, Pallas kernels: 41.9 us -> 37.6 us  [body(): pl.pallas_call(functools.partial(kernel, nz, ny, nm, 1.0 / math.sqrt(LANE...]
where the time goes in v2:
time: 39.1 us; the launch traced here: 38.9 us
  Pallas kernels  37.6 us (96%)
  local copies, waits for them, and re-layouts  1.32 us (3%)
    pallas_call x1, Pallas kernels, body(): pl.pallas_call(functools.partial(kernel, nz, ny, nm, 1.0 / math.sqrt(LANE...  37.6 us
    unnamed x1, local copies, waits for them, and re-layouts  1.32 us

profile of v2, /device:TPU:1, one launch (start us, length us, event | category | flops | bytes accessed | tf_op | source)
XLA Modules:
  0.0 38.9 jit_solution(15365067517116966413)
XLA Ops:
  0.0 37.6 %spilled_attention.1 = bf16[32,256]{1,0:T(8,128)(2,1)} custom-call(bf16[64,128]{1,0:T(8,128)(2,1)} %bitcast.9, bf16[8,256,128]{2,1,0:T(8,128)(2,1)} %bitcast.8, bf16[32,256,128]{2,1,0:T(8,128)(2,1)} %bitcast.7, bf16[64,128]{1,0:T(8,128)(2,1)} %bitcast.10, bf16[64,128]{1,0:T(8,128)(2,1)} %bitcast.11, s32[1,256]{1,0:T(1,128)} %bitcast.13, ...), custom_call_target="tpu_custom_call" | custom-call | tf_op jit(solution)/shard_map/spilled_attention/pallas_call | solution.py:472
  37.6 1.3 %copy.10 = bf16[32,256]{1,0:T(8,128)(2,1)} copy(bf16[32,256]{1,0:T(8,128)(2,1)} %spilled_attention.1) | data formatting | bytes 32768

commit v3 on v2

--- a/solution.py
+++ b/solution.py
@@ -134,8 +134,8 @@
 
     near_first = distance_order(nz)
     far_first = near_first[::-1]
-    serve_batches = [[0]] + batches([dz for dz in far_first if dz], (2, 2, 3))
-    project_batches = [[0]] + batches([dz for dz in near_first if dz], (3, 4))
+    serve_batches = [[0]] + batches([dz for dz in far_first if dz], (1, 2, 2, 2))
+    project_batches = [[0]] + batches([dz for dz in far_first if dz], (4, 3))
 
     def batch_of(dz, cut):
         return next(i for i, batch in enumerate(cut) if dz in batch)
@@ -205,14 +205,11 @@
     row_lane = iota((rows, LANES), 1)
     same_head = row_lane // SEQS == row % HEADS
     picks = jnp.where(same_head, dot(expand, picked.astype(bf16)), 0.0).astype(bf16)
-    chosen[pl.ds(0, rows), :] = picks
 
     home_row, home_lane = iota((64, LANES), 0), iota((64, LANES), 1)
     turned = ones_where(
         (home_lane // SEQS == home_row % HEADS) & (home_lane % SEQS == home_row // HEADS)
     )
-    chosen[pl.ds(rows, 64), :] = turned
-    chosen[pl.ds(rows + 64, 64), :] = turned
     queries = q_ref[...]
     by_head = dot_first(turned, queries).astype(bf16)
     q_send[...] = dot(picks, by_head).astype(bf16).reshape(groups, SLOTS * HEADS, LANES)
@@ -313,6 +310,10 @@
             mixed.append(o[0:8] + o[8:16])
         return best, sums, jnp.concatenate(mixed, axis=0)
 
+    square = ones_where(home_row == home_lane)
+    chosen[:, pl.ds(0, rows)] = dot_last(square, picks)
+    turned_back = dot_last(square, turned)
+    chosen[:, pl.ds(rows, 128)] = jnp.concatenate([turned_back, turned_back], axis=1)
     small[5].wait()
     wide_count = jnp.concatenate([home_count] * (home_tokens // LANES), axis=1)
     best, sums, mixed = partials(queries, [resident[k] for k in range(SEQS)], wide_count)
@@ -359,13 +360,16 @@
 
     many(p_send, p_recv, groups - 1, ps_sem.at[0], pr_sem.at[0]).wait_recv()
     parts = p_recv[...].reshape(rows + 128, LANES)
-    peaks = dot(parts, ones_where(iota((LANES, LANES), 0) < 3))
-    member = chosen[...].astype(f32) > 0.5
-    peak = jnp.max(jnp.where(member, peaks, very_low), axis=0, keepdims=True)
+    peaks = dot_last(ones_where(iota((SEQS, LANES), 1) < 3), parts)
+    peaks = jnp.broadcast_to(peaks[0:1], chosen.shape)
+    member = chosen[...] > 0.5
+    peak = jnp.max(jnp.where(member, peaks, very_low), axis=1, keepdims=True)
     factor = jnp.where(member, jnp.exp(peaks - peak), 0.0)
-    factor_top = factor.astype(bf16)
-    factor_low = (factor - factor_top.astype(f32)).astype(bf16)
-    merged = (dot_first(factor_top, parts) + dot_first(factor_low, parts))[0:64]
+    factor_top = rounded(factor)
+    merged = dot(
+        jnp.concatenate([factor_top, factor - factor_top], axis=0).astype(bf16), parts
+    )
+    merged = merged[0:64] + merged[64:128]
     merged_sum = merged[:, 3:4] + merged[:, 4:5] + merged[:, 5:6]
     latent = merged / merged_sum
     low_lane = iota((SEQS, LANES), 1) < RANK
@@ -471,7 +475,7 @@
     dma = pltpu.SemaphoreType.DMA
     return pl.pallas_call(
         functools.partial(kernel, nz, ny, nm, 1.0 / math.sqrt(LANES)),
-        out_shape=jax.ShapeDtypeStruct((ny * SEQS, out_columns), bf16),
+        out_shape=pltpu.VMEM((ny * SEQS, out_columns), bf16),
         in_specs=[anywhere] * 8,
         out_specs=in_vmem,
         scratch_shapes=[
@@ -485,7 +489,7 @@
             pltpu.VMEM(out_weight.shape, bf16),
             pltpu.VMEM((HEADS * RANK, out_columns), bf16),
             pltpu.VMEM((HEADS * RANK, out_columns), bf16),
-            pltpu.VMEM((rows + 128, LANES), bf16),
+            pltpu.VMEM((SEQS * HEADS, rows + 128), f32),
             pltpu.VMEM((rows, LANES), f32),
             pltpu.VMEM((groups, SLOTS * HEADS, LANES), bf16),
             pltpu.VMEM((groups, SLOTS * HEADS, LANES), bf16),
@@ -496,10 +500,10 @@
             pltpu.VMEM((ny * SEQS, out_columns), f32),
             pltpu.VMEM((nm, ny * SEQS, out_columns), bf16),
             pltpu.VMEM((nm, ny * SEQS, out_columns), bf16),
-            dma((4,)),
+            dma((5,)),
             dma((7,)),
             dma((1,)),
-            dma((4,)),
+            dma((5,)),
             dma((1,)),
             dma((1,)),
             dma((1,)),

time: 39.1 us -> 37.9 us (0.969)
  local copies, waits for them, and re-layouts: 1.32 us -> 0.61 us
  Pallas kernels: 37.6 us -> 37.2 us
    unnamed x1, local copies, waits for them, and re-layouts: 1.32 us -> 0.61 us
    pallas_call x1, Pallas kernels: 37.6 us -> 37.2 us  [body(): pl.pallas_call(functools.partial(kernel, nz, ny, nm, 1.0 / math.sqrt(LANE...]
where the time goes in v3:
time: 37.9 us; the launch traced here: 37.8 us
  Pallas kernels  37.2 us (98%)
  local copies, waits for them, and re-layouts  0.61 us (2%)
    pallas_call x1, Pallas kernels, body(): pl.pallas_call(functools.partial(kernel, nz, ny, nm, 1.0 / math.sqrt(LANE...  37.2 us

profile of v3, /device:TPU:1, one launch (start us, length us, event | category | flops | bytes accessed | tf_op | source)
XLA Modules:
  0.0 37.8 jit_solution(4428897312972172587)
XLA Ops:
  0.0 37.2 %spilled_attention.1 = bf16[32,256]{1,0:T(8,128)(2,1)S(1)} custom-call(bf16[64,128]{1,0:T(8,128)(2,1)} %bitcast.9, bf16[8,256,128]{2,1,0:T(8,128)(2,1)} %bitcast.8, bf16[32,256,128]{2,1,0:T(8,128)(2,1)} %bitcast.7, bf16[64,128]{1,0:T(8,128)(2,1)} %bitcast.10, bf16[64,128]{1,0:T(8,128)(2,1)} %bitcast.11, s32[1,256]{1,0:T(1,128)} %bitcast.13, ...), custom_call_target="tpu_custom_call" | custom-call | tf_op jit(solution)/shard_map/spilled_attention/pallas_call | solution.py:476
  37.2 0.6 %copy.10 = bf16[32,256]{1,0:T(8,128)(2,1)} copy(bf16[32,256]{1,0:T(8,128)(2,1)S(1)} %spilled_attention.1) | data formatting | bytes 32768

commit v4 on v3

--- a/solution.py
+++ b/solution.py
@@ -84,6 +84,8 @@
     rt_ref,
     pages,
     resident,
+    keys,
+    values,
     wbuf,
     w_top,
     w_low,
@@ -134,7 +136,7 @@
 
     near_first = distance_order(nz)
     far_first = near_first[::-1]
-    serve_batches = [[0]] + batches([dz for dz in far_first if dz], (1, 2, 2, 2))
+    serve_batches = [[0]] + batches([dz for dz in far_first if dz], (4, 3))
     project_batches = [[0]] + batches([dz for dz in far_first if dz], (4, 3))
 
     def batch_of(dz, cut):
@@ -329,12 +331,55 @@
         w_top[pl.ds(h * RANK, RANK), :] = joined.astype(bf16)
         w_low[pl.ds(h * RANK, RANK), :] = (joined - rounded(joined)).astype(bf16)
 
-    chunk = ny * SLOTS * HEADS
+    pick_keys = ones_where(iota((RANK, LANES), 0) == iota((RANK, LANES), 1))
     for i, batch in enumerate(serve_batches):
         held = len(batch) * ny
         pltpu.make_async_copy(
             ovf_ref.at[pl.ds(0, held)], pages.at[pl.ds(0, held)], page_sem.at[i]
         ).wait()
+        for slot in [dz * ny + ya for dz in batch for ya in range(ny)]:
+            page_pair = pages[slot]
+            turned_keys = dot_last(pick_keys, page_pair).astype(bf16)
+            keys[slot, pl.ds(0, RANK), :] = turned_keys[:, 0:PAGE]
+            keys[slot, pl.ds(RANK, RANK), :] = turned_keys[:, PAGE : 2 * PAGE]
+            values[slot] = jnp.concatenate(
+                [page_pair[PAGE : 2 * PAGE, RANK:], page_pair[0:PAGE, RANK:]], axis=1
+            )
+
+    wk_twice = jnp.concatenate([wk_ref[...], wk_ref[...]], axis=0)
+
+    def served(query_rows, slots, token_count):
+        at, row_at = iota(query_rows.shape, 1), iota(query_rows.shape, 0)
+        second = (row_at // HEADS) % SLOTS == 1
+        folded = dot_last(query_rows, wk_twice)
+        folded = jnp.where((at >= RANK) == second, folded, 0.0)
+        top = folded.astype(bf16)
+        rest = folded - top.astype(f32)
+        middle = rest.astype(bf16)
+        low = (rest - middle.astype(f32)).astype(bf16)
+        scores = []
+        for i, slot in enumerate(slots):
+            part = slice(16 * i, 16 * i + 16)
+            s = dot(jnp.concatenate([top[part], middle[part], low[part]], axis=0), keys[slot])
+            scores.append(s[0:16] + s[16:32] + s[32:48])
+        scores = jnp.concatenate(scores, axis=0) * scale
+        mask = at.astype(f32) < token_count
+        scores = jnp.where(mask, scores, very_low)
+        best = jnp.max(scores, axis=1, keepdims=True)
+        weights = jnp.where(mask, jnp.exp(scores - best), 0.0)
+        sums = jnp.sum(weights, axis=1, keepdims=True)
+        top = weights.astype(bf16)
+        low = (weights - top.astype(f32)).astype(bf16)
+        mixed = []
+        for i, slot in enumerate(slots):
+            part = slice(16 * i, 16 * i + 16)
+            o = dot(jnp.concatenate([top[part], low[part]], axis=0), values[slot])
+            mixed.append(o[0:16] + o[16:32])
+        mixed = jnp.concatenate(mixed, axis=0)
+        return best, sums, jnp.where(second, pltpu.roll(mixed, RANK, 1), mixed)
+
+    chunk = ny * SLOTS * HEADS
+    for i, batch in enumerate(serve_batches):
         many(q_send, q_recv, slots_in(batch), qs_sem.at[0], qr_sem.at[i]).wait_recv()
         block = jnp.concatenate(
             [q_recv[pl.ds(dz * ny, ny)].reshape(chunk, LANES) for dz in batch], axis=0
@@ -342,12 +387,8 @@
         token_count = jnp.concatenate(
             [counts[pl.ds(dz * chunk, chunk), :] for dz in batch], axis=0
         )
-        latents = [
-            pages[dz * ny + i // SLOTS, pl.ds((i % SLOTS) * PAGE, PAGE), :]
-            for dz in batch
-            for i in range(ny * SLOTS)
-        ]
-        best, sums, mixed = partials(block, latents, token_count)
+        slots = [dz * ny + ya for dz in batch for ya in range(ny)]
+        best, sums, mixed = served(block, slots, token_count)
         packed, _ = message(best, sums, mixed)
         packed = packed.astype(bf16).reshape(len(batch) * ny, SLOTS * HEADS, LANES)
         for n, dz in enumerate(batch):
@@ -486,6 +527,8 @@
             pltpu.VMEM((tail, 1, total), i32),
             pltpu.VMEM((groups, SLOTS * PAGE, LANES), bf16),
             pltpu.VMEM((SEQS, home_tokens, LANES), bf16),
+            pltpu.VMEM((groups, SLOTS * RANK, PAGE), bf16),
+            pltpu.VMEM((groups, PAGE, SLOTS * RANK), bf16),
             pltpu.VMEM(out_weight.shape, bf16),
             pltpu.VMEM((HEADS * RANK, out_columns), bf16),
             pltpu.VMEM((HEADS * RANK, out_columns), bf16),

time: 37.9 us -> 37.2 us (0.982)
  Pallas kernels: 37.2 us -> 36.5 us
    pallas_call x1, Pallas kernels: 37.2 us -> 36.5 us  [body(): pl.pallas_call(functools.partial(kernel, nz, ny, nm, 1.0 / math.sqrt(LANE...]
where the time goes in v4:
time: 37.2 us; the launch traced here: 37.1 us
  Pallas kernels  36.5 us (98%)
  local copies, waits for them, and re-layouts  0.61 us (2%)
    pallas_call x1, Pallas kernels, body(): pl.pallas_call(functools.partial(kernel, nz, ny, nm, 1.0 / math.sqrt(LANE...  36.5 us

profile of v4, /device:TPU:1, one launch (start us, length us, event | category | flops | bytes accessed | tf_op | source)
XLA Modules:
  0.0 37.1 jit_solution(848651498823970134)
XLA Ops:
  0.0 36.5 %spilled_attention.1 = bf16[32,256]{1,0:T(8,128)(2,1)S(1)} custom-call(bf16[64,128]{1,0:T(8,128)(2,1)} %bitcast.9, bf16[8,256,128]{2,1,0:T(8,128)(2,1)} %bitcast.8, bf16[32,256,128]{2,1,0:T(8,128)(2,1)} %bitcast.7, bf16[64,128]{1,0:T(8,128)(2,1)} %bitcast.10, bf16[64,128]{1,0:T(8,128)(2,1)} %bitcast.11, s32[1,256]{1,0:T(1,128)} %bitcast.13, ...), custom_call_target="tpu_custom_call" | custom-call | tf_op jit(solution)/shard_map/spilled_attention/pallas_call | solution.py:517
  36.5 0.6 %copy.10 = bf16[32,256]{1,0:T(8,128)(2,1)} copy(bf16[32,256]{1,0:T(8,128)(2,1)S(1)} %spilled_attention.1) | data formatting | bytes 32768

commit v5 on v4

--- a/solution.py
+++ b/solution.py
@@ -110,10 +110,14 @@
     ar_sem,
     rs_sem,
     rr_sem,
+    ws_sem,
+    wr_sem,
 ):
     me, mp = lax.axis_index("dp"), lax.axis_index("mp")
     z, y = lax.div(me, ny), lax.rem(me, ny)
     groups = nz * ny
+    core, partner = lax.rem(mp, 2), mp + 1
+    half = nm // 2
     items = groups * SLOTS
     rows = items * HEADS
     tail = rt_ref.shape[0]
@@ -328,8 +332,23 @@
     small[6].wait()
     for h in range(HEADS):
         joined = dot(wv_ref[...], wbuf[pl.ds(h * LANES, LANES), :])
-        w_top[pl.ds(h * RANK, RANK), :] = joined.astype(bf16)
-        w_low[pl.ds(h * RANK, RANK), :] = (joined - rounded(joined)).astype(bf16)
+        w_top[core, pl.ds(h * RANK, RANK), :] = joined.astype(bf16)
+        w_low[core, pl.ds(h * RANK, RANK), :] = (joined - rounded(joined)).astype(bf16)
+
+    def weight_handover(which, array):
+        return pltpu.make_async_remote_copy(
+            src_ref=array.at[0],
+            dst_ref=array.at[0],
+            send_sem=ws_sem.at[which],
+            recv_sem=wr_sem.at[which],
+            device_id=(me, partner),
+            device_id_type=MESH,
+        )
+
+    @pl.when(core == 0)
+    def _():
+        weight_handover(0, w_top).start()
+        weight_handover(1, w_low).start()
 
     pick_keys = ones_where(iota((RANK, LANES), 0) == iota((RANK, LANES), 1))
     for i, batch in enumerate(serve_batches):
@@ -424,40 +443,50 @@
     def latent_copy(dz, peer):
         return pltpu.make_async_remote_copy(
             src_ref=own_lat,
-            dst_ref=all_lat.at[me],
+            dst_ref=all_lat.at[core * groups + me],
             send_sem=as_sem.at[0],
             recv_sem=ar_sem.at[batch_of(dz, project_batches)],
-            device_id=(peer, mp),
+            device_id=(peer, lax.div(mp, 2) * 2 + 1),
             device_id_type=MESH,
         )
 
     for dz in far_first:
         for ya in others_in_plane(dz):
             latent_copy(dz, holder_at(dz, ya)).start()
-    all_lat[me] = own_lat[...]
+
+    @pl.when(core == 0)
+    def _():
+        latent_copy(0, me).start()
+
+    @pl.when(core == 1)
+    def _():
+        all_lat[groups + me] = own_lat[...]
 
     def sum_copy(target):
+        place = lax.rem(lax.div(mp, 2) + half - lax.div(target, 2), half)
         return pltpu.make_async_remote_copy(
             src_ref=r_send.at[target],
-            dst_ref=r_recv.at[lax.rem(mp + nm - target, nm)],
+            dst_ref=r_recv.at[place],
             send_sem=rs_sem.at[0],
             recv_sem=rr_sem.at[0],
             device_id=(me, target),
             device_id_type=MESH,
         )
 
-    for i, batch in enumerate(project_batches):
-        many(all_lat, all_lat, slots_in(batch), as_sem.at[0], ar_sem.at[i]).wait_recv()
-        block = jnp.concatenate(
-            [
-                all_lat[pl.ds(lax.rem(z + nz - dz, nz) * ny, ny)].reshape(
-                    ny * SEQS, HEADS * RANK
-                )
-                for dz in batch
-            ],
-            axis=0,
-        )
-        part = dot(block, w_top[...]) + dot(block, w_low[...])
+    def project(batch):
+        part = None
+        for c in range(2):
+            block = jnp.concatenate(
+                [
+                    all_lat[
+                        pl.ds(c * groups + lax.rem(z + nz - dz, nz) * ny, ny)
+                    ].reshape(ny * SEQS, HEADS * RANK)
+                    for dz in batch
+                ],
+                axis=0,
+            )
+            added = dot(block, w_top[c]) + dot(block, w_low[c])
+            part = added if part is None else part + added
         for n, dz in enumerate(batch):
             target = lax.rem(z + nz - dz, nz)
             piece = part[n * ny * SEQS : (n + 1) * ny * SEQS]
@@ -471,15 +500,38 @@
                 r_send[target] = piece.astype(bf16)
                 sum_copy(target).start()
 
-    many(r_send, r_recv, nm - 1, rs_sem.at[0], rr_sem.at[0]).wait_recv()
+    @pl.when(core == 1)
+    def _():
+        weight_handover(0, w_top).wait_recv()
+        weight_handover(1, w_low).wait_recv()
+        for i, batch in enumerate(project_batches):
+            landed = slots_in(batch) + len(batch) * ny
+            many(all_lat, all_lat, landed, as_sem.at[0], ar_sem.at[i]).wait_recv()
+            project(batch)
+        many(r_send, r_recv, half - 1, rs_sem.at[0], rr_sem.at[0]).wait_recv()
+
+    @pl.when(core == 0)
+    def _():
+        many(r_send, r_recv, half, rs_sem.at[0], rr_sem.at[0]).wait_recv()
+        own_part[...] = r_recv[0].astype(f32)
+
     summed = own_part[...]
-    for step in range(1, nm):
-        summed = summed + r_recv[step].astype(f32)
+    for place in range(1, half):
+        summed = summed + r_recv[place].astype(f32)
     out_ref[...] = summed.astype(bf16)
     many(q_send, q_recv, groups - 1, qs_sem.at[0], qr_sem.at[0]).wait_send()
     many(p_send, p_recv, groups - 1, ps_sem.at[0], pr_sem.at[0]).wait_send()
-    many(all_lat, all_lat, groups - 1, as_sem.at[0], ar_sem.at[0]).wait_send()
-    many(r_send, r_recv, nm - 1, rs_sem.at[0], rr_sem.at[0]).wait_send()
+
+    @pl.when(core == 0)
+    def _():
+        weight_handover(0, w_top).wait_send()
+        weight_handover(1, w_low).wait_send()
+        many(all_lat, all_lat, groups, as_sem.at[0], ar_sem.at[0]).wait_send()
+
+    @pl.when(core == 1)
+    def _():
+        many(all_lat, all_lat, groups - 1, as_sem.at[0], ar_sem.at[0]).wait_send()
+        many(r_send, r_send, nm - 1, rs_sem.at[0], rr_sem.at[0]).wait_send()
 
 
 def body(
@@ -530,8 +582,8 @@
             pltpu.VMEM((groups, SLOTS * RANK, PAGE), bf16),
             pltpu.VMEM((groups, PAGE, SLOTS * RANK), bf16),
             pltpu.VMEM(out_weight.shape, bf16),
-            pltpu.VMEM((HEADS * RANK, out_columns), bf16),
-            pltpu.VMEM((HEADS * RANK, out_columns), bf16),
+            pltpu.VMEM((2, HEADS * RANK, out_columns), bf16),
+            pltpu.VMEM((2, HEADS * RANK, out_columns), bf16),
             pltpu.VMEM((SEQS * HEADS, rows + 128), f32),
             pltpu.VMEM((rows, LANES), f32),
             pltpu.VMEM((groups, SLOTS * HEADS, LANES), bf16),
@@ -539,10 +591,10 @@
             pltpu.VMEM((groups, SLOTS * HEADS, LANES), bf16),
             pltpu.VMEM((groups + 8, SLOTS * HEADS, LANES), bf16),
             pltpu.VMEM((SEQS, HEADS * RANK), bf16),
-            pltpu.VMEM((groups, SEQS, HEADS * RANK), bf16),
+            pltpu.VMEM((2 * groups, SEQS, HEADS * RANK), bf16),
             pltpu.VMEM((ny * SEQS, out_columns), f32),
             pltpu.VMEM((nm, ny * SEQS, out_columns), bf16),
-            pltpu.VMEM((nm, ny * SEQS, out_columns), bf16),
+            pltpu.VMEM((nm // 2, ny * SEQS, out_columns), bf16),
             dma((5,)),
             dma((7,)),
             dma((1,)),
@@ -553,6 +605,8 @@
             dma((3,)),
             dma((1,)),
             dma((1,)),
+            dma((2,)),
+            dma((2,)),
         ],
         compiler_params=pltpu.CompilerParams(collective_id=0, has_side_effects=True),
         name="spilled_attention",

time: 37.2 us -> 36.4 us (0.978)
  Pallas kernels: 36.5 us -> 35.7 us
    pallas_call x1, Pallas kernels: 36.5 us -> 35.7 us  [body(): pl.pallas_call(functools.partial(kernel, nz, ny, nm, 1.0 / math.sqrt(LANE...]
where the time goes in v5:
time: 36.4 us; the launch traced here: 36.3 us
  Pallas kernels  35.7 us (98%)
  local copies, waits for them, and re-layouts  0.61 us (2%)
    pallas_call x1, Pallas kernels, body(): pl.pallas_call(functools.partial(kernel, nz, ny, nm, 1.0 / math.sqrt(LANE...  35.7 us

profile of v5, /device:TPU:1, one launch (start us, length us, event | category | flops | bytes accessed | tf_op | source)
XLA Modules:
  0.0 36.3 jit_solution(8601744643086651320)
XLA Ops:
  0.0 35.7 %spilled_attention.1 = bf16[32,256]{1,0:T(8,128)(2,1)S(1)} custom-call(bf16[64,128]{1,0:T(8,128)(2,1)} %bitcast.9, bf16[8,256,128]{2,1,0:T(8,128)(2,1)} %bitcast.8, bf16[32,256,128]{2,1,0:T(8,128)(2,1)} %bitcast.7, bf16[64,128]{1,0:T(8,128)(2,1)} %bitcast.10, bf16[64,128]{1,0:T(8,128)(2,1)} %bitcast.11, s32[1,256]{1,0:T(1,128)} %bitcast.13, ...), custom_call_target="tpu_custom_call" | custom-call | tf_op jit(solution)/shard_map/spilled_attention/pallas_call | solution.py:569
  35.7 0.6 %copy.10 = bf16[32,256]{1,0:T(8,128)(2,1)} copy(bf16[32,256]{1,0:T(8,128)(2,1)S(1)} %spilled_attention.1) | data formatting | bytes 32768

commit v6 on v5

--- a/solution.py
+++ b/solution.py
@@ -51,7 +51,7 @@
 
 
 def distance_order(nz):
-    return sorted(range(nz), key=lambda dz: (min(dz, nz - dz), dz))
+    return sorted(range(nz), key=lambda dz: (min(dz, nz - dz), -dz))
 
 
 def batches(order, sizes):
@@ -141,7 +141,7 @@
     near_first = distance_order(nz)
     far_first = near_first[::-1]
     serve_batches = [[0]] + batches([dz for dz in far_first if dz], (4, 3))
-    project_batches = [[0]] + batches([dz for dz in far_first if dz], (4, 3))
+    project_batches = batches(near_first, (1, 1, 2, 2, 2))
 
     def batch_of(dz, cut):
         return next(i for i, batch in enumerate(cut) if dz in batch)
@@ -445,18 +445,28 @@
             src_ref=own_lat,
             dst_ref=all_lat.at[core * groups + me],
             send_sem=as_sem.at[0],
-            recv_sem=ar_sem.at[batch_of(dz, project_batches)],
+            recv_sem=ar_sem.at[dz],
             device_id=(peer, lax.div(mp, 2) * 2 + 1),
             device_id_type=MESH,
         )
 
-    for dz in far_first:
-        for ya in others_in_plane(dz):
-            latent_copy(dz, holder_at(dz, ya)).start()
+    to_first = lax.rem(nz - z, nz)
 
     @pl.when(core == 0)
     def _():
         latent_copy(0, me).start()
+
+    @pl.when(z != 0)
+    def _():
+        for ya in range(ny):
+            latent_copy(to_first, ya).start()
+
+    for dz in near_first:
+
+        @pl.when((to_first != dz) | (dz == 0))
+        def _():
+            for ya in others_in_plane(dz):
+                latent_copy(dz, holder_at(dz, ya)).start()
 
     @pl.when(core == 1)
     def _():
@@ -504,9 +514,10 @@
     def _():
         weight_handover(0, w_top).wait_recv()
         weight_handover(1, w_low).wait_recv()
-        for i, batch in enumerate(project_batches):
-            landed = slots_in(batch) + len(batch) * ny
-            many(all_lat, all_lat, landed, as_sem.at[0], ar_sem.at[i]).wait_recv()
+        for batch in project_batches:
+            for dz in batch:
+                landed = slots_in([dz]) + ny
+                many(all_lat, all_lat, landed, as_sem.at[0], ar_sem.at[dz]).wait_recv()
             project(batch)
         many(r_send, r_recv, half - 1, rs_sem.at[0], rr_sem.at[0]).wait_recv()
 
@@ -602,7 +613,7 @@
             dma((1,)),
             dma((1,)),
             dma((1,)),
-            dma((3,)),
+            dma((nz,)),
             dma((1,)),
             dma((1,)),
             dma((2,)),

time: 36.4 us -> 34 us (0.934)
  the two profiles are of different devices: /device:TPU:1 before, /device:TPU:38 now
where the time goes in v6:
time: 34 us; the launch traced here: 33.9 us
  Pallas kernels  33.3 us (98%)
  local copies, waits for them, and re-layouts  0.61 us (2%)
    pallas_call x1, Pallas kernels, body(): pl.pallas_call(functools.partial(kernel, nz, ny, nm, 1.0 / math.sqrt(LANE...  33.3 us

profile of v6, /device:TPU:38, one launch (start us, length us, event | category | flops | bytes accessed | tf_op | source)
XLA Modules:
  0.0 33.9 jit_solution(18006288360997780863)
XLA Ops:
  0.0 33.3 %spilled_attention.1 = bf16[32,256]{1,0:T(8,128)(2,1)S(1)} custom-call(bf16[64,128]{1,0:T(8,128)(2,1)} %bitcast.9, bf16[8,256,128]{2,1,0:T(8,128)(2,1)} %bitcast.8, bf16[32,256,128]{2,1,0:T(8,128)(2,1)} %bitcast.7, bf16[64,128]{1,0:T(8,128)(2,1)} %bitcast.10, bf16[64,128]{1,0:T(8,128)(2,1)} %bitcast.11, s32[1,256]{1,0:T(1,128)} %bitcast.13, ...), custom_call_target="tpu_custom_call" | custom-call | tf_op jit(solution)/shard_map/spilled_attention/pallas_call | solution.py:580
  33.3 0.6 %copy.10 = bf16[32,256]{1,0:T(8,128)(2,1)} copy(bf16[32,256]{1,0:T(8,128)(2,1)S(1)} %spilled_attention.1) | data formatting | bytes 32768

commit v7 on v6

--- a/solution.py
+++ b/solution.py
@@ -450,20 +450,23 @@
             device_id_type=MESH,
         )
 
-    to_first = lax.rem(nz - z, nz)
+    early = [lax.rem(nz + plane - z, nz) for plane in range(min(3, nz))]
 
     @pl.when(core == 0)
     def _():
         latent_copy(0, me).start()
 
-    @pl.when(z != 0)
-    def _():
-        for ya in range(ny):
-            latent_copy(to_first, ya).start()
+    for plane, to_plane in enumerate(early):
+
+        @pl.when(z != plane)
+        def _():
+            for ya in range(ny):
+                latent_copy(to_plane, plane * ny + ya).start()
 
     for dz in near_first:
-
-        @pl.when((to_first != dz) | (dz == 0))
+        later = functools.reduce(jnp.logical_and, [to_plane != dz for to_plane in early])
+
+        @pl.when(later | (dz == 0))
         def _():
             for ya in others_in_plane(dz):
                 latent_copy(dz, holder_at(dz, ya)).start()

time: 34 us -> 33.4 us (0.982)
  the two profiles are of different devices: /device:TPU:38 before, /device:TPU:1 now
where the time goes in v7:
time: 33.4 us; the launch traced here: 33.2 us
  Pallas kernels  32.5 us (97%)
  local copies, waits for them, and re-layouts  0.61 us (2%)
    pallas_call x1, Pallas kernels, body(): pl.pallas_call(functools.partial(kernel, nz, ny, nm, 1.0 / math.sqrt(LANE...  32.5 us

profile of v7, /device:TPU:1, one launch (start us, length us, event | category | flops | bytes accessed | tf_op | source)
XLA Modules:
  0.0 33.2 jit_solution(9633257390786388231)
XLA Ops:
  0.0 32.5 %spilled_attention.1 = bf16[32,256]{1,0:T(8,128)(2,1)S(1)} custom-call(bf16[64,128]{1,0:T(8,128)(2,1)} %bitcast.9, bf16[8,256,128]{2,1,0:T(8,128)(2,1)} %bitcast.8, bf16[32,256,128]{2,1,0:T(8,128)(2,1)} %bitcast.7, bf16[64,128]{1,0:T(8,128)(2,1)} %bitcast.10, bf16[64,128]{1,0:T(8,128)(2,1)} %bitcast.11, s32[1,256]{1,0:T(1,128)} %bitcast.13, ...), custom_call_target="tpu_custom_call" | custom-call | tf_op jit(solution)/shard_map/spilled_attention/pallas_call | solution.py:583
  32.6 0.6 %copy.10 = bf16[32,256]{1,0:T(8,128)(2,1)} copy(bf16[32,256]{1,0:T(8,128)(2,1)S(1)} %spilled_attention.1) | data formatting | bytes 32768

commit v8 on v7

--- a/solution.py
+++ b/solution.py
@@ -141,7 +141,7 @@
     near_first = distance_order(nz)
     far_first = near_first[::-1]
     serve_batches = [[0]] + batches([dz for dz in far_first if dz], (4, 3))
-    project_batches = batches(near_first, (1, 1, 2, 2, 2))
+    project_batches = batches(near_first, (1, 1, 2, 2, 1, 1))
 
     def batch_of(dz, cut):
         return next(i for i, batch in enumerate(cut) if dz in batch)
@@ -445,7 +445,7 @@
             src_ref=own_lat,
             dst_ref=all_lat.at[core * groups + me],
             send_sem=as_sem.at[0],
-            recv_sem=ar_sem.at[dz],
+            recv_sem=ar_sem.at[core * nz + dz],
             device_id=(peer, lax.div(mp, 2) * 2 + 1),
             device_id_type=MESH,
         )
@@ -463,7 +463,8 @@
             for ya in range(ny):
                 latent_copy(to_plane, plane * ny + ya).start()
 
-    for dz in near_first:
+    upward_first = [*range(nz // 2), *range(nz - 1, nz // 2 - 1, -1)]
+    for dz in upward_first:
         later = functools.reduce(jnp.logical_and, [to_plane != dz for to_plane in early])
 
         @pl.when(later | (dz == 0))
@@ -488,7 +489,12 @@
 
     def project(batch):
         part = None
-        for c in range(2):
+        for c in (1, 0):
+            for dz in batch:
+                landed = slots_in([dz]) if c else ny
+                many(
+                    all_lat, all_lat, landed, as_sem.at[0], ar_sem.at[c * nz + dz]
+                ).wait_recv()
             block = jnp.concatenate(
                 [
                     all_lat[
@@ -518,9 +524,6 @@
         weight_handover(0, w_top).wait_recv()
         weight_handover(1, w_low).wait_recv()
         for batch in project_batches:
-            for dz in batch:
-                landed = slots_in([dz]) + ny
-                many(all_lat, all_lat, landed, as_sem.at[0], ar_sem.at[dz]).wait_recv()
             project(batch)
         many(r_send, r_recv, half - 1, rs_sem.at[0], rr_sem.at[0]).wait_recv()
 
@@ -616,7 +619,7 @@
             dma((1,)),
             dma((1,)),
             dma((1,)),
-            dma((nz,)),
+            dma((2 * nz,)),
             dma((1,)),
             dma((1,)),
             dma((2,)),

time: 33.4 us -> 33.4 us (level)
  no operation moved by 1% of the time
where the time goes in v8:
time: 33.4 us; the launch traced here: 33.1 us
  Pallas kernels  32.5 us (97%)
  local copies, waits for them, and re-layouts  0.61 us (2%)
    pallas_call x1, Pallas kernels, body(): pl.pallas_call(functools.partial(kernel, nz, ny, nm, 1.0 / math.sqrt(LANE...  32.5 us

profile of v8, /device:TPU:1, one launch (start us, length us, event | category | flops | bytes accessed | tf_op | source)
XLA Modules:
  0.0 33.1 jit_solution(1618040186202405700)
XLA Ops:
  0.0 32.5 %spilled_attention.1 = bf16[32,256]{1,0:T(8,128)(2,1)S(1)} custom-call(bf16[64,128]{1,0:T(8,128)(2,1)} %bitcast.9, bf16[8,256,128]{2,1,0:T(8,128)(2,1)} %bitcast.8, bf16[32,256,128]{2,1,0:T(8,128)(2,1)} %bitcast.7, bf16[64,128]{1,0:T(8,128)(2,1)} %bitcast.10, bf16[64,128]{1,0:T(8,128)(2,1)} %bitcast.11, s32[1,256]{1,0:T(1,128)} %bitcast.13, ...), custom_call_target="tpu_custom_call" | custom-call | tf_op jit(solution)/shard_map/spilled_attention/pallas_call | solution.py:586
  32.5 0.6 %copy.10 = bf16[32,256]{1,0:T(8,128)(2,1)} copy(bf16[32,256]{1,0:T(8,128)(2,1)S(1)} %spilled_attention.1) | data formatting | bytes 32768

commit v9 on v7

--- a/solution.py
+++ b/solution.py
@@ -116,7 +116,7 @@
     me, mp = lax.axis_index("dp"), lax.axis_index("mp")
     z, y = lax.div(me, ny), lax.rem(me, ny)
     groups = nz * ny
-    core, partner = lax.rem(mp, 2), mp + 1
+    core = lax.rem(mp, 2)
     half = nm // 2
     items = groups * SLOTS
     rows = items * HEADS
@@ -341,7 +341,7 @@
             dst_ref=array.at[0],
             send_sem=ws_sem.at[which],
             recv_sem=wr_sem.at[which],
-            device_id=(me, partner),
+            device_id=(me, lax.div(mp, 2) * 2 + 1),
             device_id_type=MESH,
         )
 

time: 33.4 us -> 33.4 us (level)
  no operation moved by 1% of the time
where the time goes in v9:
time: 33.4 us; the launch traced here: 33.2 us
  Pallas kernels  32.5 us (97%)
  local copies, waits for them, and re-layouts  0.61 us (2%)
    pallas_call x1, Pallas kernels, body(): pl.pallas_call(functools.partial(kernel, nz, ny, nm, 1.0 / math.sqrt(LANE...  32.5 us

profile of v9, /device:TPU:1, one launch (start us, length us, event | category | flops | bytes accessed | tf_op | source)
XLA Modules:
  0.0 33.2 jit_solution(1508588858015471054)
XLA Ops:
  0.0 32.5 %spilled_attention.1 = bf16[32,256]{1,0:T(8,128)(2,1)S(1)} custom-call(bf16[64,128]{1,0:T(8,128)(2,1)} %bitcast.9, bf16[8,256,128]{2,1,0:T(8,128)(2,1)} %bitcast.8, bf16[32,256,128]{2,1,0:T(8,128)(2,1)} %bitcast.7, bf16[64,128]{1,0:T(8,128)(2,1)} %bitcast.10, bf16[64,128]{1,0:T(8,128)(2,1)} %bitcast.11, s32[1,256]{1,0:T(1,128)} %bitcast.13, ...), custom_call_target="tpu_custom_call" | custom-call | tf_op jit(solution)/shard_map/spilled_attention/pallas_call | solution.py:583
  32.6 0.6 %copy.10 = bf16[32,256]{1,0:T(8,128)(2,1)} copy(bf16[32,256]{1,0:T(8,128)(2,1)S(1)} %spilled_attention.1) | data formatting | bytes 32768
